TPU v7x, 128 devices: a whole 4x4x4 slice. The times are simulated.
128 devices in a mesh: shard: 16 (over z_hi, x, core), tp: 8 (over z_lo, y).
Axes of the slice: x: 4, y: 4, z: 4 (z_hi: 2, z_lo: 2; z = z_hi * 2 + z_lo), core: 2. Of those that a mesh axis runs over, the one named last changes fastest.
Arguments:
- train_query: bfloat16 [5120, 8192], P('shard', 'tp'), may hold values from -0.078125 to 0.078125
- low_query: bfloat16 [5120, 32], P('shard'), may hold values from -0.078125 to 0.078125
- high_query: bfloat16 [32, 8192], P(None, 'tp'), may hold values from -1 to 1
- train_key: bfloat16 [5120, 1024], P('shard', 'tp'), may hold values from -0.078125 to 0.078125
- low_key: bfloat16 [5120, 32], P('shard'), may hold values from -0.078125 to 0.078125
- high_key: bfloat16 [32, 1024], P(None, 'tp'), may hold values from -1 to 1
- train_value: bfloat16 [5120, 1024], P('shard', 'tp'), may hold values from -0.078125 to 0.078125
- low_value: bfloat16 [5120, 32], P('shard'), may hold values from -0.078125 to 0.078125
- high_value: bfloat16 [32, 1024], P(None, 'tp'), may hold values from -1 to 1
- train_mixed: bfloat16 [8192, 5120], P('tp', 'shard'), may hold values from -0.0625 to 0.0625
- low_mixed: bfloat16 [8192, 32], P('tp'), may hold values from -0.0625 to 0.0625
- high_mixed: bfloat16 [32, 5120], P(None, 'shard'), may hold values from -1 to 1
- norm_train: float32 [5120], P(('shard', 'tp')), may hold values from 0.25 to 1.75
- norm_step: float32 [5120], P(('shard', 'tp')), may hold values from -0.3 to 0.3
Outputs:
- final_query: bfloat16 [5120, 8192], P(None, 'tp')
- final_key: bfloat16 [5120, 1024], P(None, 'tp')
- final_value: bfloat16 [5120, 1024], P(None, 'tp')
- final_mixed: bfloat16 [8192, 5120], P('tp')
- serve_norm: bfloat16 [5120], replicated
All inputs are finite; a program needn't handle non-finite values.
Results may differ from a plain program's by a relative error of at most 0.001.
Values may be sent and summed in bfloat16 or wider, within the bound.
A program may use at most 128 MiB of HBM per device.

v0:
```python
import jax
import jax.numpy as jnp
from jax import lax
from jax.sharding import PartitionSpec as P

mix_rate = 0.5


def rows_first(arrays, axis, dims):
    turned = [jnp.moveaxis(a, dim, 0) for a, dim in zip(arrays, dims)]
    widths = [t[0].size for t in turned]
    both = jnp.concatenate([t.reshape(-1, w) for t, w in zip(turned, widths)], axis=1)
    out = lax.all_gather(both, axis, axis=0, tiled=True)
    parts = jnp.split(out, [sum(widths[:k]) for k in range(1, len(widths))], axis=1)
    return tuple(
        (
            jnp.moveaxis(b.reshape(-1, *t.shape[1:]), 0, dim)
            for b, t, dim in zip(parts, turned, dims)
        )
    )


def body(
    train_query,
    low_query,
    high_query,
    train_key,
    low_key,
    high_key,
    train_value,
    low_value,
    high_value,
    train_mixed,
    low_mixed,
    high_mixed,
    norm_train,
    norm_step,
):
    result_query = train_query.astype(jnp.float32) + mix_rate * jnp.dot(
        low_query, high_query, preferred_element_type=jnp.float32
    )
    result_key = train_key.astype(jnp.float32) + mix_rate * jnp.dot(
        low_key, high_key, preferred_element_type=jnp.float32
    )
    result_value = train_value.astype(jnp.float32) + mix_rate * jnp.dot(
        low_value, high_value, preferred_element_type=jnp.float32
    )
    result_mixed = train_mixed.astype(jnp.float32) + mix_rate * jnp.dot(
        low_mixed, high_mixed, preferred_element_type=jnp.float32
    )
    narrow_query, narrow_key, narrow_value, narrow_mixed = (
        result_query.astype(jnp.bfloat16),
        result_key.astype(jnp.bfloat16),
        result_value.astype(jnp.bfloat16),
        result_mixed.astype(jnp.bfloat16),
    )
    final_query, final_key, final_value, final_mixed = rows_first(
        (narrow_query, narrow_key, narrow_value, narrow_mixed), "shard", (0, 0, 0, 1)
    )
    serve_norm = lax.all_gather(
        (norm_train + norm_step).astype(jnp.bfloat16), ("shard", "tp"), axis=0, tiled=True
    )
    return (final_query, final_key, final_value, final_mixed, serve_norm)


def solution(mesh):
    return jax.shard_map(
        body,
        mesh=mesh,
        in_specs=(
            P("shard", "tp"),
            P("shard", None),
            P(None, "tp"),
            P("shard", "tp"),
            P("shard", None),
            P(None, "tp"),
            P("shard", "tp"),
            P("shard", None),
            P(None, "tp"),
            P("tp", "shard"),
            P("tp", None),
            P(None, "shard"),
            P(("shard", "tp")),
            P(("shard", "tp")),
        ),
        out_specs=(P(None, "tp"), P(None, "tp"), P(None, "tp"), P("tp", None), P()),
        check_vma=False,
    )
```

profile of v0, /device:TPU:1, one launch (start us, length us, event | category | flops | bytes accessed | tf_op | source)
XLA Modules:
  0.0 198.9 jit_solution(14225677418639521225)
XLA Ops:
  7.2 0.0 copy-start
  7.2 0.0 copy-start.4
  7.2 0.0 copy-start.6
  7.2 0.0 copy-start.2
  7.2 0.0 copy-start.5
  7.2 0.0 copy-start.3
  7.2 0.0 copy-start.1
  7.2 0.0 all-gather.2.cloned.1.call-start
  7.3 0.7 copy-done
  8.0 1.5 fusion.4
  9.5 1.1 fusion.8
  10.6 0.0 copy-done.4
  10.7 0.2 fusion.7
  10.9 0.4 fusion.2
  11.3 1.2 pad_maximum_fusion
  12.5 0.0 all-gather.2.cloned.1.call-update
  12.5 0.6 copy-done.7
  13.1 0.0 copy-done.8
  13.2 0.2 dynamic-update-slice
  13.4 139.6 %all-reduce = bf16[5120]{0:T(1024)(128)(2,1)} all-reduce(bf16[5120]{0:T(1024)(128)(2,1)S(1)} %dynamic-update-slice), channel_id=1, replica_groups=mesh['shard'=16,'tp'=8] {'shard','tp'}, use_global_device_ids=true, to_apply=%add | all-reduce | flops 5120 | bytes 20480
  153.0 5.9 %all-gather.2.cloned.1.call-done = bf16[5120,2304]{1,0:T(8,128)(2,1)} async-done(((bf16[320,2304]{1,0:T(8,128)(2,1)}), bf16[5120,2304]{1,0:T(8,128)(2,1)}) %all-gather.2.cloned.1.call-update) | async-done | bytes 23592976 | tf_op jit(solution)/shard_map/all_gather | solution.py:13
  158.8 16.2 %slice_bitcast_fusion = (bf16[1024,5120]{0,1:T(8,128)(2,1)}, bf16[5120,1024]{1,0:T(8,128)(2,1)}) fusion(bf16[5120,2304]{1,0:T(8,128)(2,1)} %all-gather.2.cloned.1.call-done), kind=kLoop, calls=%fused_computation | loop fusion | bytes 41943040 | tf_op jit(solution)/shard_map/transpose | solution.py:17
  175.0 13.7 %copy.19 = bf16[1024,5120]{1,0:T(8,128)(2,1)} copy(bf16[1024,5120]{0,1:T(8,128)(2,1)} %get-tuple-element.10) | data formatting | bytes 20971520
  188.7 3.4 %fusion.9 = (bf16[5120,128]{1,0:T(8,128)(2,1)}, bf16[5120,128]{1,0:T(8,128)(2,1)}) fusion(bf16[5120,2304]{1,0:T(8,128)(2,1)} %all-gather.2.cloned.1.call-done), kind=kLoop, calls=%fused_computation.16 | loop fusion | bytes 5242880 | tf_op jit(solution)/shard_map/split | solution.py:14
  (9 shorter events, 0.0 us)
Async XLA Ops:
  7.2 0.8 copy-start
  7.2 3.4 %copy-start.4 = (bf16[320,32]{0,1:T(8,128)(2,1)S(1)}, bf16[320,32]{0,1:T(8,128)(2,1)}, u32[]{:S(2)}) copy-start(bf16[320,32]{0,1:T(8,128)(2,1)} %param.18) | copy-start | bytes 61444
  7.2 3.4 %copy-start.6 = (bf16[32,128]{1,0:T(8,128)(2,1)S(1)}, bf16[32,128]{1,0:T(8,128)(2,1)}, u32[]{:S(2)}) copy-start(bf16[32,128]{1,0:T(8,128)(2,1)} %param.19) | copy-start | bytes 24580
  7.2 3.4 %copy-start.2 = (bf16[320,128]{1,0:T(8,128)(2,1)S(1)}, bf16[320,128]{1,0:T(8,128)(2,1)}, u32[]{:S(2)}) copy-start(bf16[320,128]{1,0:T(8,128)(2,1)} %param.17) | copy-start | bytes 245764
  7.2 3.7 %copy-start.5 = (bf16[320,32]{0,1:T(8,128)(2,1)S(1)}, bf16[320,32]{0,1:T(8,128)(2,1)}, u32[]{:S(2)}) copy-start(bf16[320,32]{0,1:T(8,128)(2,1)} %param.15) | copy-start | bytes 61444
  7.2 3.7 %copy-start.3 = (bf16[32,1024]{1,0:T(8,128)(2,1)S(1)}, bf16[32,1024]{1,0:T(8,128)(2,1)}, u32[]{:S(2)}) copy-start(bf16[32,1024]{1,0:T(8,128)(2,1)} %param.16) | copy-start | bytes 196612
  7.2 3.7 %copy-start.1 = (bf16[320,1024]{1,0:T(8,128)(2,1)S(1)}, bf16[320,1024]{1,0:T(8,128)(2,1)}, u32[]{:S(2)}) copy-start(bf16[320,1024]{1,0:T(8,128)(2,1)} %param.14) | copy-start | bytes 1966084
  7.2 151.6 %all-gather.2.cloned.1.call-start = ((), (), s32[]{:S(2)}) async-start(), calls=%async_computation | async-start | bytes 25067520 | tf_op jit(solution)/shard_map/all_gather | solution.py:13
  12.5 0.7 copy-start.7
  12.5 0.7 copy-start.8
Sparse Core Ops, SparseCore 0:
  12.6 146.1 all-gather.1
where the time goes:
time: 200 us; the launch traced here: 199 us
  blocking collectives  140 us (70%)
  local copies, waits for them, and re-layouts  34.9 us (17%)
  between operations  14.2 us (7%)
  waiting for transfers between devices  5.87 us (3%)
  matrix products  3.16 us (2%)
    unnamed x1, blocking collectives  140 us
    transpose x1, local copies, waits for them, and re-layouts, rows_first(): jnp.moveaxis(b.reshape(-1, *t.shape[1:]), 0, dim)  16.2 us
    unnamed x21, local copies, waits for them, and re-layouts  15.3 us
    all_gather x1, waiting for transfers between devices, rows_first(): out = lax.all_gather(both, axis, axis=0, tiled=True)  5.85 us
  transfers between devices with their start and end apart: 1, of which 1 were waited for; matrix products, arithmetic and copies ran while one was open for 0% of the time, Pallas kernels for 0%

commit v1 on v0

v1 whole, which is shorter than its diff:
```python
import functools
import heapq

import jax
import jax.numpy as jnp
from jax import lax
from jax.experimental import pallas as pl
from jax.experimental.pallas import tpu as pltpu
from jax.sharding import PartitionSpec as P

MESH = pl.DeviceIdType.MESH
mix_rate = 0.5

Q_ROWS = 80
M_ROWS = 128
HALF = (0, 0, 0, 1, 1, 1, 0, 0, 1, 1)
IS_B = (0,) * 6 + (1,) * 4
SIZES = (163840, 163840, 81920, 163840, 163840, 81920) + (163840,) * 4
N_CHUNKS = 10
RELAY_SLOT = {0: 0, 1: 1, 2: 2, 3: 0, 4: 1, 5: 2}


def own_sends(chunk, along_x, along_z):
    sends = []
    if along_z:
        sends.append(("z+", ("r+", 0, chunk)) if HALF[chunk] == 0 else ("z-", ("r-", 0, chunk)))
    if along_x:
        sends += [("x+", ("x+", 0, 3, chunk)), ("x-", ("x-", 0, 1, chunk))]
    if along_z:
        sends.append(("d", ("d", 0, 0, chunk)))
    return sends


def react(event):
    kind = event[0]
    if kind in ("r+", "r-"):
        return [("z" + kind[1], ("z",) + event[1:])]
    if kind == "z":
        _, dx, chunk = event
        sends = [("d", ("d", 1, dx, chunk))]
        if not IS_B[chunk]:
            sends += [("x+", ("x+", 1, 3, chunk)), ("x-", ("x-", 1, 1, chunk))]
        return sends
    _, dz, dx, chunk = event
    sends = []
    if kind == "x+" and dx == 3 and HALF[chunk] == 0:
        sends.append(("x+", ("x+", dz, 2, chunk)))
    if kind == "x-" and dx == 1 and HALF[chunk] == 1:
        sends.append(("x-", ("x-", dz, 2, chunk)))
    if IS_B[chunk] and dz == 0:
        sends.append(("z+", ("r+", dx, chunk)) if HALF[chunk] == 0 else ("z-", ("r-", dx, chunk)))
    sends.append(("d", ("d", dz, dx, chunk)))
    return sends


def plan():
    first = []
    for chunk in (0, 3):
        first += own_sends(chunk, True, True)
    second = []
    for chunk in (1, 4, 2, 5):
        second += own_sends(chunk, False, True)
    third = []
    for chunk in (6, 8, 7, 9):
        third += own_sends(chunk, True, True)
    for chunk in (1, 4, 2, 5):
        third += own_sends(chunk, True, False)
    starts = [(3.5, first), (4.0, second), (8.0, third)]
    heap, count, free, order = [], 0, {}, []
    for time, sends in starts:
        heapq.heappush(heap, (time, count, None, sends))
        count += 1
    while heap:
        time, _, event, sends = heapq.heappop(heap)
        if event is not None:
            order.append((time, event))
            sends = react(event)
        for link, item in sends:
            if link == "d":
                continue
            done = max(time, free.get(link, 0.0)) + SIZES[item[-1]] / 45000.0
            free[link] = done
            heapq.heappush(heap, (done + 1.9, count, item, None))
            count += 1
    order += [(9.0, ("ny",)), (32.0, ("nz",)), (56.0, ("nx",))]
    order = [event for _, event in sorted(order, key=lambda pair: pair[0])]
    return first, second, third, order


def count_sends():
    first, second, third, order = plan()
    total = len(first) + len(second) + len(third)
    for event in order:
        if event[0][0] != "n":
            total += len(react(event))
    return total + 2 + 3 + 3 + 3 + 4


N_SENDS = count_sends()
N_LOADS = 14


def gather_kernel(
    tq, lq, hq, tk, lk, hk, tv, lv, hv, tm, lm, hm, n1, n2,
    q_all, k_all, v_all, m_all, n_all,
    tq_v, lq_v, hq_v, tk_v, lk_v, hk_v, tv_v, lv_v, hv_v, tm_v, lm_v, hm_v, n1_v, n2_v,
    tm_s, hm_s, turn, relay_q, relay_kv, relay_m,
    load_sem, send_sem, arrive_sem, relay_sem, sib_sem, pair_sem, norm_sem,
):
    sh = lax.axis_index("shard")
    tp = lax.axis_index("tp")
    core = lax.rem(sh, 2)
    x = lax.rem(sh // 2, 4)
    z = (sh // 8) * 2 + tp // 4
    y = lax.rem(tp, 4)

    def device(dx=0, dz=0, dy=0, other=False):
        zz = lax.rem(z + dz, 4)
        cc = 1 - core if other else core
        return (
            ((zz // 2) * 4 + lax.rem(x + dx, 4)) * 2 + cc,
            lax.rem(zz, 2) * 4 + lax.rem(y + dy, 4),
        )

    target = {
        "x+": device(dx=1), "x-": device(dx=3), "z+": device(dz=1), "z-": device(dz=3), "d": device(other=True),
    }

    loads = []
    for k, (src, dst) in enumerate((
        (tq, tq_v), (lq, lq_v), (hq, hq_v), (tm, tm_v), (hm, hm_v), (lm, lm_v), (tk, tk_v), (lk, lk_v), (hk, hk_v),
        (tv, tv_v), (lv, lv_v), (hv, hv_v), (n1, n1_v), (n2, n2_v),
    )):
        copy = pltpu.make_async_copy(src, dst, load_sem.at[k])
        copy.start()
        loads.append(copy)

    partners = [device(dx=k) for k in (1, 2, 3)] + [device(dz=k) for k in (1, 2, 3)]
    partners += [device(dy=k) for k in (1, 2, 3)] + [device(other=True)]
    barrier = pltpu.get_barrier_semaphore()
    for partner in partners:
        pl.semaphore_signal(barrier, inc=1, device_id=partner, device_id_type=MESH)
    pl.semaphore_wait(barrier, len(partners))

    started = []

    def send(src, dst, sem, to):
        copy = pltpu.make_async_remote_copy(
            src_ref=src, dst_ref=dst, send_sem=send_sem.at[len(started)], recv_sem=sem,
            device_id=to, device_id_type=MESH,
        )
        copy.start()
        started.append(copy)

    def arrived(dst, sem):
        pltpu.make_async_remote_copy(
            src_ref=dst, dst_ref=dst, send_sem=send_sem.at[0], recv_sem=sem,
            device_id=target["d"], device_id_type=MESH,
        ).wait_recv()

    def place(chip, cc, chunk):
        row = (chip * 2 + cc) * 320
        if chunk in (2, 5):
            return (k_all if chunk == 2 else v_all).at[pl.ds(pl.multiple_of(row, 64), 320)]
        if chunk < 6:
            part = chunk if chunk < 2 else chunk - 1
            return q_all.at[pl.ds(pl.multiple_of(row + Q_ROWS * part, 16), Q_ROWS)]
        return m_all.at[chip, pl.ds(pl.multiple_of(512 * cc + M_ROWS * (chunk - 6), M_ROWS), M_ROWS)]

    def chip_at(dz2, dx):
        return (lax.rem(sh // 8 + dz2, 2)) * 4 + lax.rem(x + dx, 4)

    def relay_place(way, dx, chunk):
        if chunk in (2, 5):
            return relay_kv.at[way]
        if chunk < 6:
            return relay_q.at[way, pl.ds(Q_ROWS * (chunk % 3), Q_ROWS)]
        return relay_m.at[way, dx, pl.ds(M_ROWS * (chunk % 2), M_ROWS)]

    def relay_index(way, dx, chunk):
        return way * 11 + (chunk % 3 if chunk < 6 else 3 + dx * 2 + chunk % 2)

    def arrive_index(dz, dx, chunk):
        return (dz * 4 + dx) * N_CHUNKS + chunk

    def dispatch(link, item, src, chip):
        kind, chunk = item[0], item[-1]
        if kind in ("r+", "r-"):
            way = HALF[chunk]
            dst, sem = relay_place(way, item[1], chunk), relay_sem.at[relay_index(way, item[1], chunk)]
        elif kind == "d":
            dst, sem = src, sib_sem.at[arrive_index(item[1], item[2], chunk)]
        elif kind == "z":
            dst, sem = place(chip, core, chunk), arrive_sem.at[arrive_index(1, item[1], chunk)]
        else:
            dst, sem = src, arrive_sem.at[arrive_index(item[1], item[2], chunk)]
        send(src, dst, sem, target[link])

    first, second, third, order = plan()
    own = chip_at(0, 0)

    def wait_loads(*which):
        for k in which:
            loads[k].wait()

    half = pl.ds(pl.multiple_of(512 * core, 512), 512)
    other_half = pl.ds(pl.multiple_of(512 * (1 - core), 512), 512)
    wait_loads(3, 4)
    send(tm_v.at[:, other_half], tm_s, pair_sem.at[0], target["d"])
    send(hm_v, hm_s, pair_sem.at[1], target["d"])

    def product(low_turned, high):
        return mix_rate * lax.dot_general(
            low_turned, high, (((0,), (0,)), ((), ())), preferred_element_type=jnp.float32
        )

    row = sh * 320
    wait_loads(0, 1, 2)
    q_all[pl.ds(pl.multiple_of(row, 64), 320)] = (
        tq_v[...].astype(jnp.float32) + product(lq_v[...], hq_v[...])
    ).astype(jnp.bfloat16)
    wait_loads(12, 13)
    n_at = (x * 2 + core) * 4 + z
    n_all[n_at, y] = jnp.zeros((1, 128), jnp.float32)
    n_all[n_at, y, :, 0:40] = n1_v[...] + n2_v[...]
    for link, item in first:
        dispatch(link, item, place(own, core, item[-1]), own)
    wait_loads(6, 7, 8, 9, 10, 11)
    k_all[pl.ds(pl.multiple_of(row, 64), 320)] = (
        tk_v[...].astype(jnp.float32) + product(lk_v[...], hk_v[...])
    ).astype(jnp.bfloat16)
    v_all[pl.ds(pl.multiple_of(row, 64), 320)] = (
        tv_v[...].astype(jnp.float32) + product(lv_v[...], hv_v[...])
    ).astype(jnp.bfloat16)
    for k in (1, 2, 3):
        send(n_all.at[n_at, y], n_all.at[n_at, y], norm_sem.at[k - 1], device(dy=k))
    for link, item in second:
        dispatch(link, item, place(own, core, item[-1]), own)

    wait_loads(5)
    arrived(tm_s, pair_sem.at[0])
    arrived(hm_s, pair_sem.at[1])
    mine = pl.ds(pl.multiple_of(320 * core, 64), 320)
    others = pl.ds(pl.multiple_of(320 * (1 - core), 64), 320)
    low_half = lm_v[:, half]
    own_half = tm_v[:, half]
    for b in range(4):
        cols = slice(M_ROWS * b, M_ROWS * (b + 1))
        low = low_half[:, cols]
        turn[b, mine] = own_half[:, cols].astype(jnp.float32) + product(hm_v[...], low)
        turn[b, others] = tm_s[:, cols].astype(jnp.float32) + product(hm_s[...], low)
        rows = pl.ds(pl.multiple_of(512 * core + M_ROWS * b, M_ROWS), M_ROWS)
        m_all[own, rows] = turn[b].T.astype(jnp.bfloat16)
    for link, item in third:
        dispatch(link, item, place(own, core, item[-1]), own)

    for event in order:
        kind, chunk = event[0], event[-1]
        if kind == "ny":
            for k in (1, 2, 3):
                arrived(n_all.at[n_at, lax.rem(y + 4 - k, 4)], norm_sem.at[k - 1])
            for k in (1, 2, 3):
                send(n_all.at[n_at], n_all.at[n_at], norm_sem.at[3 + k - 1], device(dz=k))
        elif kind == "nz":
            block = (x * 2 + core) * 4
            for k in (1, 2, 3):
                arrived(n_all.at[block + lax.rem(z + 4 - k, 4)], norm_sem.at[3 + k - 1])
            line = n_all.at[pl.ds(block, 4)]
            for k in (1, 2, 3):
                send(line, line, norm_sem.at[6 + k - 1], device(dx=k))
            send(line, line, norm_sem.at[9], target["d"])
        elif kind == "nx":
            for k in (1, 2, 3):
                line = n_all.at[pl.ds((lax.rem(x + 4 - k, 4) * 2 + core) * 4, 4)]
                arrived(line, norm_sem.at[6 + k - 1])
                send(line, line, norm_sem.at[9 + k], target["d"])
        elif kind in ("r+", "r-"):
            way = HALF[chunk]
            src = relay_place(way, event[1], chunk)
            arrived(src, relay_sem.at[relay_index(way, event[1], chunk)])
            from_z = lax.rem(z + (3 if way == 0 else 1), 4)
            chip = (from_z // 2) * 4 + lax.rem(x + event[1], 4)
            for link, item in react(event):
                dispatch(link, item, src, chip)
        else:
            dz, dx = (1, event[1]) if kind == "z" else (event[1], event[2])
            chip = chip_at(dz, dx)
            src = place(chip, core, chunk)
            arrived(src, arrive_sem.at[arrive_index(dz, dx, chunk)])
            for link, item in react(event):
                dispatch(link, item, src, chip)

    for dz in (0, 1):
        for dx in range(4):
            for chunk in range(N_CHUNKS):
                arrived(place(chip_at(dz, dx), 1 - core, chunk), sib_sem.at[arrive_index(dz, dx, chunk)])
    for k in range(4):
        line = n_all.at[pl.ds((lax.rem(x + 4 - k, 4) * 2 + 1 - core) * 4, 4)]
        arrived(line, norm_sem.at[9 + k])
    for copy in started:
        copy.wait_send()


def write_kernel(q_all, k_all, v_all, m_all, n_all, q_out, k_out, v_out, m_out, n_out, lines, sems):
    copies = []
    for k in range(8):
        copies.append((m_all.at[k], m_out.at[:, pl.ds(640 * k, 640)]))
        copies.append((q_all.at[pl.ds(640 * k, 640)], q_out.at[pl.ds(640 * k, 640)]))
    copies += [(k_all, k_out), (v_all, v_out)]
    copies = [pltpu.make_async_copy(src, dst, sems.at[k]) for k, (src, dst) in enumerate(copies)]
    for copy in copies:
        copy.start()
    lane = lax.broadcasted_iota(jnp.int32, (8, 128), 1)
    acc = [jnp.zeros((8, 128), jnp.float32) for _ in range(5)]
    for i in range(16):
        core, zl, y = i // 8, (i // 4) % 2, i % 4
        rows = [n_all[(xx * 2 + core) * 4 + zh * 2 + zl, y] for zh in range(2) for xx in range(4)]
        block = jnp.concatenate(rows, axis=0)
        q, off = (40 * i) // 128, (40 * i) % 128
        turned = pltpu.roll(block, off, 1) if off else block
        acc[q] = jnp.where((lane >= off) & (lane < off + 40), turned, acc[q])
        if off + 40 > 128:
            acc[q + 1] = jnp.where(lane < off + 40 - 128, turned, acc[q + 1])
    for q in range(5):
        lines[pl.ds(q, 8, stride=5), :] = acc[q]
    n_out[...] = lines[...].astype(jnp.bfloat16)
    for copy in copies:
        copy.wait()


def body(
    train_query, low_query, high_query, train_key, low_key, high_key, train_value, low_value, high_value,
    train_mixed, low_mixed, high_mixed, norm_train, norm_step,
):
    bf16, f32 = jnp.bfloat16, jnp.float32
    args = (
        train_query, low_query.T, high_query, train_key, low_key.T, high_key, train_value, low_value.T, high_value,
        train_mixed.T, low_mixed.T, high_mixed, norm_train.reshape(1, -1), norm_step.reshape(1, -1),
    )
    vmem = pltpu.MemorySpace.VMEM
    q_all, k_all, v_all, m_all, n_all = pl.pallas_call(
        gather_kernel,
        name="gather",
        out_shape=[
            vmem((5120, 1024), bf16), vmem((5120, 128), bf16), vmem((5120, 128), bf16),
            vmem((8, 1024, 640), bf16), vmem((32, 4, 1, 128), f32),
        ],
        in_specs=[pl.BlockSpec(memory_space=pltpu.MemorySpace.HBM)] * 14,
        out_specs=[pl.BlockSpec(memory_space=vmem)] * 5,
        scratch_shapes=[pltpu.VMEM(a.shape, a.dtype) for a in args] + [
            pltpu.VMEM((320, 512), bf16), pltpu.VMEM((32, 320), bf16), pltpu.VMEM((4, 640, 128), f32),
            pltpu.VMEM((2, 160, 1024), bf16), pltpu.VMEM((2, 320, 128), bf16), pltpu.VMEM((2, 4, 256, 640), bf16),
            pltpu.SemaphoreType.DMA((N_LOADS,)), pltpu.SemaphoreType.DMA((N_SENDS,)),
            pltpu.SemaphoreType.DMA((80,)), pltpu.SemaphoreType.DMA((22,)), pltpu.SemaphoreType.DMA((80,)),
            pltpu.SemaphoreType.DMA((2,)), pltpu.SemaphoreType.DMA((13,)),
        ],
        compiler_params=pltpu.CompilerParams(
            collective_id=0, has_side_effects=True, vmem_limit_bytes=36 * 1024 * 1024
        ),
    )(*args)
    hbm = pltpu.MemorySpace.HBM
    q, k, v, m, n = pl.pallas_call(
        write_kernel,
        name="write",
        out_shape=[
            jax.ShapeDtypeStruct((5120, 1024), bf16), jax.ShapeDtypeStruct((5120, 128), bf16),
            jax.ShapeDtypeStruct((5120, 128), bf16), jax.ShapeDtypeStruct((1024, 5120), bf16),
            jax.ShapeDtypeStruct((40, 128), bf16),
        ],
        in_specs=[pl.BlockSpec(memory_space=vmem)] * 5,
        out_specs=[pl.BlockSpec(memory_space=hbm)] * 4 + [pl.BlockSpec(memory_space=vmem)],
        scratch_shapes=[pltpu.VMEM((40, 128), f32), pltpu.SemaphoreType.DMA((18,))],
        compiler_params=pltpu.CompilerParams(vmem_limit_bytes=36 * 1024 * 1024),
    )(q_all, k_all, v_all, m_all, n_all)
    return q, k, v, m, n.reshape(5120)


def solution(mesh):
    return jax.shard_map(
        body,
        mesh=mesh,
        in_specs=(
            P("shard", "tp"), P("shard", None), P(None, "tp"),
            P("shard", "tp"), P("shard", None), P(None, "tp"),
            P("shard", "tp"), P("shard", None), P(None, "tp"),
            P("tp", "shard"), P("tp", None), P(None, "shard"),
            P(("shard", "tp")), P(("shard", "tp")),
        ),
        out_specs=(P(None, "tp"), P(None, "tp"), P(None, "tp"), P("tp", None), P()),
        check_vma=False,
    )
```

time: 200 us -> 108 us (0.54)
  blocking collectives: 140 us -> 0 us
  Pallas kernels: 0 us -> 103 us
  local copies, waits for them, and re-layouts: 34.9 us -> 3.96 us
  between operations: 14.2 us -> 0.65 us
  waiting for transfers between devices: 5.87 us -> 0 us
  matrix products: 3.16 us -> 0 us
    unnamed x1 -> x0, blocking collectives: 140 us -> none
    pallas_call x0 -> x2, Pallas kernels: none -> 103 us  [the longest x1 90.2 us: body(): pl.pallas_call(gather_kernel, name='gather', out_shape=[vmem((5120, 1024)...]
    transpose x1 -> x0, local copies, waits for them, and re-layouts: 16.2 us -> none  [rows_first(): jnp.moveaxis(b.reshape(-1, *t.shape[1:]), 0, dim)]
    unnamed x21 -> x2, local copies, waits for them, and re-layouts: 15.3 us -> 3.96 us
    all_gather x1 -> x0, waiting for transfers between devices: 5.85 us -> none  [rows_first(): out = lax.all_gather(both, axis, axis=0, tiled=True)]
    split x1 -> x0, local copies, waits for them, and re-layouts: 3.38 us -> none  [rows_first(): jnp.split(out, [sum(widths[:k]) for k in range(1, len(widths))], axis=1)]
    dot_general x4 -> x0, matrix products: 3.16 us -> none  [the longest x1 1.47 us: body(): jnp.dot(low_mixed, high_mixed, preferred_element_type=jnp.float32)]
  transfers between devices with their start and end apart: 1 -> 0, of which waited for: 1 -> 0; matrix products, arithmetic and copies ran while one was open for 0% -> 0% of each run, Pallas kernels for 0% -> 0%
where the time goes in v1:
time: 108 us; the launch traced here: 107 us
  Pallas kernels  103 us (95%)
  local copies, waits for them, and re-layouts  3.96 us (4%)
    pallas_call x1, Pallas kernels, body(): pl.pallas_call(gather_kernel, name='gather', out_shape=[vmem((5120, 1024)...  90.2 us
    pallas_call x1, Pallas kernels, body(): pl.pallas_call(write_kernel, name='write', out_shape=[jax.ShapeDtypeStruc...  12.7 us
    unnamed x2, local copies, waits for them, and re-layouts  3.96 us

profile of v1, /device:TPU:1, one launch (start us, length us, event | category | flops | bytes accessed | tf_op | source)
XLA Modules:
  0.0 107.4 jit_solution(16016804823003438767)
XLA Ops:
  0.6 90.2 %gather.1 = (bf16[5120,1024]{1,0:T(8,128)(2,1)S(1)}, bf16[5120,128]{1,0:T(8,128)(2,1)S(1)}, bf16[5120,128]{1,0:T(8,128)(2,1)S(1)}, bf16[8,1024,640]{2,1,0:T(8,128)(2,1)S(1)}, f32[32,4,1,128]{3,2,1,0:T(1,128)S(1)}) custom-call(bf16[320,1024]{1,0:T(8,128)(2,1)} %tq.1, bf16[32,320]{1,0:T(8,128)(2,1)} %bitcast.10, bf16[32,1024]{1,0:T(8,128)(2,1)} %hq.1, ...), custom_call_target="tpu_custom_call" | custom-call | tf_op jit(solution)/shard_map/gather/pallas_call | solution.py:341
  90.8 0.0 copy-start
  90.8 4.0 %copy-done = bf16[8,1024,640]{2,1,0:T(8,128)(2,1)} copy-done((bf16[8,1024,640]{2,1,0:T(8,128)(2,1)}, bf16[8,1024,640]{2,1,0:T(8,128)(2,1)S(1)}, u32[]{:S(2)}) %copy-start) | copy-done | bytes 10485784
  94.8 12.7 %write.1 = (bf16[5120,1024]{1,0:T(8,128)(2,1)}, bf16[5120,128]{1,0:T(8,128)(2,1)}, bf16[5120,128]{1,0:T(8,128)(2,1)}, bf16[1024,5120]{1,0:T(8,128)(2,1)}, bf16[40,128]{1,0:T(8,128)(2,1)}) custom-call(bf16[5120,1024]{1,0:T(8,128)(2,1)S(1)} %get-tuple-element.15.q_all, bf16[5120,128]{1,0:T(8,128)(2,1)S(1)} %get-tuple-element.16.k_all, ...), custom_call_target="tpu_custom_call" | custom-call | tf_op jit(solution)/shard_map/write/pallas_call | solution.py:362
Async XLA Ops:
  90.8 4.0 %copy-start = (bf16[8,1024,640]{2,1,0:T(8,128)(2,1)}, bf16[8,1024,640]{2,1,0:T(8,128)(2,1)S(1)}, u32[]{:S(2)}) copy-start(bf16[8,1024,640]{2,1,0:T(8,128)(2,1)S(1)} %get-tuple-element.18.m_all) | copy-start | bytes 31457284

commit v2 on v1

--- a/solution.py
+++ b/solution.py
@@ -370,7 +370,7 @@
         in_specs=[pl.BlockSpec(memory_space=vmem)] * 5,
         out_specs=[pl.BlockSpec(memory_space=hbm)] * 4 + [pl.BlockSpec(memory_space=vmem)],
         scratch_shapes=[pltpu.VMEM((40, 128), f32), pltpu.SemaphoreType.DMA((18,))],
-        compiler_params=pltpu.CompilerParams(vmem_limit_bytes=36 * 1024 * 1024),
+        compiler_params=pltpu.CompilerParams(vmem_limit_bytes=2 * 1024 * 1024),
     )(q_all, k_all, v_all, m_all, n_all)
     return q, k, v, m, n.reshape(5120)
 

time: 108 us -> 99.6 us (0.922)
  Pallas kernels: 103 us -> 98.8 us
  local copies, waits for them, and re-layouts: 3.96 us -> 0 us
    pallas_call x1, Pallas kernels: 12.7 us -> 8.69 us  [body(): pl.pallas_call(write_kernel, name='write', out_shape=[jax.ShapeDtypeStruc...]
    unnamed x2 -> x0, local copies, waits for them, and re-layouts: 3.96 us -> none
where the time goes in v2:
time: 99.6 us; the launch traced here: 99.5 us
  Pallas kernels  98.8 us (99%)
    pallas_call x1, Pallas kernels, body(): pl.pallas_call(gather_kernel, name='gather', out_shape=[vmem((5120, 1024)...  90.2 us
    pallas_call x1, Pallas kernels, body(): pl.pallas_call(write_kernel, name='write', out_shape=[jax.ShapeDtypeStruc...  8.69 us

profile of v2, /device:TPU:1, one launch (start us, length us, event | category | flops | bytes accessed | tf_op | source)
XLA Modules:
  0.0 99.5 jit_solution(2801040871329591519)
XLA Ops:
  0.6 90.2 %gather.1 = (bf16[5120,1024]{1,0:T(8,128)(2,1)S(1)}, bf16[5120,128]{1,0:T(8,128)(2,1)S(1)}, bf16[5120,128]{1,0:T(8,128)(2,1)S(1)}, bf16[8,1024,640]{2,1,0:T(8,128)(2,1)S(1)}, f32[32,4,1,128]{3,2,1,0:T(1,128)S(1)}) custom-call(bf16[320,1024]{1,0:T(8,128)(2,1)} %tq.1, bf16[32,320]{1,0:T(8,128)(2,1)} %bitcast.10, bf16[32,1024]{1,0:T(8,128)(2,1)} %hq.1, ...), custom_call_target="tpu_custom_call" | custom-call | tf_op jit(solution)/shard_map/gather/pallas_call | solution.py:341
  90.8 8.7 %write.1 = (bf16[5120,1024]{1,0:T(8,128)(2,1)}, bf16[5120,128]{1,0:T(8,128)(2,1)}, bf16[5120,128]{1,0:T(8,128)(2,1)}, bf16[1024,5120]{1,0:T(8,128)(2,1)}, bf16[40,128]{1,0:T(8,128)(2,1)}) custom-call(bf16[5120,1024]{1,0:T(8,128)(2,1)S(1)} %get-tuple-element.15.q_all, bf16[5120,128]{1,0:T(8,128)(2,1)S(1)} %get-tuple-element.16.k_all, ...), custom_call_target="tpu_custom_call" | custom-call | tf_op jit(solution)/shard_map/write/pallas_call | solution.py:362

commit v3 on v2

--- a/solution.py
+++ b/solution.py
@@ -17,13 +17,13 @@
 IS_B = (0,) * 6 + (1,) * 4
 SIZES = (163840, 163840, 81920, 163840, 163840, 81920) + (163840,) * 4
 N_CHUNKS = 10
-RELAY_SLOT = {0: 0, 1: 1, 2: 2, 3: 0, 4: 1, 5: 2}
+KIND = (0, 0, 1, 0, 0, 2, 3, 3, 3, 3)
 
 
 def own_sends(chunk, along_x, along_z):
     sends = []
     if along_z:
-        sends.append(("z+", ("r+", 0, chunk)) if HALF[chunk] == 0 else ("z-", ("r-", 0, chunk)))
+        sends.append(("z", ("z", 0, chunk)))
     if along_x:
         sends += [("x+", ("x+", 0, 3, chunk)), ("x-", ("x-", 0, 1, chunk))]
     if along_z:
@@ -33,8 +33,6 @@
 
 def react(event):
     kind = event[0]
-    if kind in ("r+", "r-"):
-        return [("z" + kind[1], ("z",) + event[1:])]
     if kind == "z":
         _, dx, chunk = event
         sends = [("d", ("d", 1, dx, chunk))]
@@ -48,7 +46,7 @@
     if kind == "x-" and dx == 1 and HALF[chunk] == 1:
         sends.append(("x-", ("x-", dz, 2, chunk)))
     if IS_B[chunk] and dz == 0:
-        sends.append(("z+", ("r+", dx, chunk)) if HALF[chunk] == 0 else ("z-", ("r-", dx, chunk)))
+        sends.append(("z", ("z", dx, chunk)))
     sends.append(("d", ("d", dz, dx, chunk)))
     return sends
 
@@ -65,7 +63,7 @@
         third += own_sends(chunk, True, True)
     for chunk in (1, 4, 2, 5):
         third += own_sends(chunk, True, False)
-    starts = [(3.5, first), (4.0, second), (8.0, third)]
+    starts = [(2.0, first), (2.1, second), (6.0, third)]
     heap, count, free, order = [], 0, {}, []
     for time, sends in starts:
         heapq.heappush(heap, (time, count, None, sends))
@@ -87,16 +85,6 @@
     return first, second, third, order
 
 
-def count_sends():
-    first, second, third, order = plan()
-    total = len(first) + len(second) + len(third)
-    for event in order:
-        if event[0][0] != "n":
-            total += len(react(event))
-    return total + 2 + 3 + 3 + 3 + 4
-
-
-N_SENDS = count_sends()
 N_LOADS = 14
 
 
@@ -104,8 +92,8 @@
     tq, lq, hq, tk, lk, hk, tv, lv, hv, tm, lm, hm, n1, n2,
     q_all, k_all, v_all, m_all, n_all,
     tq_v, lq_v, hq_v, tk_v, lk_v, hk_v, tv_v, lv_v, hv_v, tm_v, lm_v, hm_v, n1_v, n2_v,
-    tm_s, hm_s, turn, relay_q, relay_kv, relay_m,
-    load_sem, send_sem, arrive_sem, relay_sem, sib_sem, pair_sem, norm_sem,
+    tm_s, hm_s, turn,
+    load_sem, send_sem, arrive_sem, sib_sem, pair_sem, norm_sem,
 ):
     sh = lax.axis_index("shard")
     tp = lax.axis_index("tp")
@@ -123,8 +111,14 @@
         )
 
     target = {
-        "x+": device(dx=1), "x-": device(dx=3), "z+": device(dz=1), "z-": device(dz=3), "d": device(other=True),
+        "x+": device(dx=1), "x-": device(dx=3), "z": device(dz=2), "d": device(other=True),
     }
+
+    partners = [device(dx=k) for k in (1, 2, 3)] + [device(dz=k) for k in (1, 2, 3)]
+    partners += [device(dy=k) for k in (1, 2, 3)] + [device(other=True)]
+    barrier = pltpu.get_barrier_semaphore()
+    for partner in partners:
+        pl.semaphore_signal(barrier, inc=1, device_id=partner, device_id_type=MESH)
 
     loads = []
     for k, (src, dst) in enumerate((
@@ -135,28 +129,31 @@
         copy.start()
         loads.append(copy)
 
-    partners = [device(dx=k) for k in (1, 2, 3)] + [device(dz=k) for k in (1, 2, 3)]
-    partners += [device(dy=k) for k in (1, 2, 3)] + [device(other=True)]
-    barrier = pltpu.get_barrier_semaphore()
-    for partner in partners:
-        pl.semaphore_signal(barrier, inc=1, device_id=partner, device_id_type=MESH)
-    pl.semaphore_wait(barrier, len(partners))
-
-    started = []
-
-    def send(src, dst, sem, to):
+    def send(src, dst, sent, sem, to):
         copy = pltpu.make_async_remote_copy(
-            src_ref=src, dst_ref=dst, send_sem=send_sem.at[len(started)], recv_sem=sem,
-            device_id=to, device_id_type=MESH,
+            src_ref=src, dst_ref=dst, send_sem=sent, recv_sem=sem, device_id=to, device_id_type=MESH,
         )
         copy.start()
-        started.append(copy)
+        return copy
+
+    def waiting(ref, sent, sem):
+        return pltpu.make_async_remote_copy(
+            src_ref=ref, dst_ref=ref, send_sem=sent, recv_sem=sem, device_id=target["d"], device_id_type=MESH,
+        )
 
     def arrived(dst, sem):
-        pltpu.make_async_remote_copy(
-            src_ref=dst, dst_ref=dst, send_sem=send_sem.at[0], recv_sem=sem,
-            device_id=target["d"], device_id_type=MESH,
-        ).wait_recv()
+        waiting(dst, send_sem.at[0], sem).wait_recv()
+
+    n_sent = [[0, 0] for _ in range(4)]
+
+    def many(kind, count):
+        if kind == 0:
+            return q_all.at[pl.ds(0, Q_ROWS * count)]
+        if kind < 3:
+            return (k_all if kind == 1 else v_all).at[pl.ds(0, 320 * count)]
+        if count % 8 == 0:
+            return m_all.at[pl.ds(0, count // 8)]
+        return m_all.at[pl.ds(0, count // 4), pl.ds(0, 512)]
 
     def place(chip, cc, chunk):
         row = (chip * 2 + cc) * 320
@@ -170,31 +167,18 @@
     def chip_at(dz2, dx):
         return (lax.rem(sh // 8 + dz2, 2)) * 4 + lax.rem(x + dx, 4)
 
-    def relay_place(way, dx, chunk):
-        if chunk in (2, 5):
-            return relay_kv.at[way]
-        if chunk < 6:
-            return relay_q.at[way, pl.ds(Q_ROWS * (chunk % 3), Q_ROWS)]
-        return relay_m.at[way, dx, pl.ds(M_ROWS * (chunk % 2), M_ROWS)]
-
-    def relay_index(way, dx, chunk):
-        return way * 11 + (chunk % 3 if chunk < 6 else 3 + dx * 2 + chunk % 2)
-
     def arrive_index(dz, dx, chunk):
         return (dz * 4 + dx) * N_CHUNKS + chunk
 
     def dispatch(link, item, src, chip):
-        kind, chunk = item[0], item[-1]
-        if kind in ("r+", "r-"):
-            way = HALF[chunk]
-            dst, sem = relay_place(way, item[1], chunk), relay_sem.at[relay_index(way, item[1], chunk)]
-        elif kind == "d":
-            dst, sem = src, sib_sem.at[arrive_index(item[1], item[2], chunk)]
-        elif kind == "z":
-            dst, sem = place(chip, core, chunk), arrive_sem.at[arrive_index(1, item[1], chunk)]
+        kind, chunk = KIND[item[-1]], item[-1]
+        if link == "d":
+            sem, side = sib_sem.at[kind], 1
         else:
-            dst, sem = src, arrive_sem.at[arrive_index(item[1], item[2], chunk)]
-        send(src, dst, sem, target[link])
+            dz, dx = (1, item[1]) if link == "z" else (item[1], item[2])
+            sem, side = arrive_sem.at[arrive_index(dz, dx, chunk)], 0
+        n_sent[kind][side] += 1
+        send(src, src, send_sem.at[kind * 2 + side], sem, target[link])
 
     first, second, third, order = plan()
     own = chip_at(0, 0)
@@ -202,12 +186,6 @@
     def wait_loads(*which):
         for k in which:
             loads[k].wait()
-
-    half = pl.ds(pl.multiple_of(512 * core, 512), 512)
-    other_half = pl.ds(pl.multiple_of(512 * (1 - core), 512), 512)
-    wait_loads(3, 4)
-    send(tm_v.at[:, other_half], tm_s, pair_sem.at[0], target["d"])
-    send(hm_v, hm_s, pair_sem.at[1], target["d"])
 
     def product(low_turned, high):
         return mix_rate * lax.dot_general(
@@ -219,12 +197,6 @@
     q_all[pl.ds(pl.multiple_of(row, 64), 320)] = (
         tq_v[...].astype(jnp.float32) + product(lq_v[...], hq_v[...])
     ).astype(jnp.bfloat16)
-    wait_loads(12, 13)
-    n_at = (x * 2 + core) * 4 + z
-    n_all[n_at, y] = jnp.zeros((1, 128), jnp.float32)
-    n_all[n_at, y, :, 0:40] = n1_v[...] + n2_v[...]
-    for link, item in first:
-        dispatch(link, item, place(own, core, item[-1]), own)
     wait_loads(6, 7, 8, 9, 10, 11)
     k_all[pl.ds(pl.multiple_of(row, 64), 320)] = (
         tk_v[...].astype(jnp.float32) + product(lk_v[...], hk_v[...])
@@ -232,12 +204,27 @@
     v_all[pl.ds(pl.multiple_of(row, 64), 320)] = (
         tv_v[...].astype(jnp.float32) + product(lv_v[...], hv_v[...])
     ).astype(jnp.bfloat16)
+    wait_loads(12, 13)
+    n_at = (x * 2 + core) * 4 + z
+    n_all[n_at, y] = jnp.zeros((1, 128), jnp.float32)
+    n_all[n_at, y, :, 0:40] = n1_v[...] + n2_v[...]
+    wait_loads(3, 4, 5)
+    pl.semaphore_wait(barrier, len(partners))
+
+    half = pl.ds(pl.multiple_of(512 * core, 512), 512)
+    other_half = pl.ds(pl.multiple_of(512 * (1 - core), 512), 512)
+    small = [
+        send(tm_v.at[:, other_half], tm_s, pair_sem.at[2], pair_sem.at[0], target["d"]),
+        send(hm_v, hm_s, pair_sem.at[3], pair_sem.at[1], target["d"]),
+    ]
+    for link, item in first:
+        dispatch(link, item, place(own, core, item[-1]), own)
     for k in (1, 2, 3):
-        send(n_all.at[n_at, y], n_all.at[n_at, y], norm_sem.at[k - 1], device(dy=k))
+        line = n_all.at[n_at, y]
+        small.append(send(line, line, norm_sem.at[12 + k], norm_sem.at[k - 1], device(dy=k)))
     for link, item in second:
         dispatch(link, item, place(own, core, item[-1]), own)
 
-    wait_loads(5)
     arrived(tm_s, pair_sem.at[0])
     arrived(hm_s, pair_sem.at[1])
     mine = pl.ds(pl.multiple_of(320 * core, 64), 320)
@@ -260,28 +247,21 @@
             for k in (1, 2, 3):
                 arrived(n_all.at[n_at, lax.rem(y + 4 - k, 4)], norm_sem.at[k - 1])
             for k in (1, 2, 3):
-                send(n_all.at[n_at], n_all.at[n_at], norm_sem.at[3 + k - 1], device(dz=k))
+                line = n_all.at[n_at]
+                small.append(send(line, line, norm_sem.at[15 + k], norm_sem.at[3 + k - 1], device(dz=k)))
         elif kind == "nz":
             block = (x * 2 + core) * 4
             for k in (1, 2, 3):
                 arrived(n_all.at[block + lax.rem(z + 4 - k, 4)], norm_sem.at[3 + k - 1])
             line = n_all.at[pl.ds(block, 4)]
             for k in (1, 2, 3):
-                send(line, line, norm_sem.at[6 + k - 1], device(dx=k))
-            send(line, line, norm_sem.at[9], target["d"])
+                small.append(send(line, line, norm_sem.at[18 + k], norm_sem.at[6 + k - 1], device(dx=k)))
+            small.append(send(line, line, norm_sem.at[22], norm_sem.at[9], target["d"]))
         elif kind == "nx":
             for k in (1, 2, 3):
                 line = n_all.at[pl.ds((lax.rem(x + 4 - k, 4) * 2 + core) * 4, 4)]
                 arrived(line, norm_sem.at[6 + k - 1])
-                send(line, line, norm_sem.at[9 + k], target["d"])
-        elif kind in ("r+", "r-"):
-            way = HALF[chunk]
-            src = relay_place(way, event[1], chunk)
-            arrived(src, relay_sem.at[relay_index(way, event[1], chunk)])
-            from_z = lax.rem(z + (3 if way == 0 else 1), 4)
-            chip = (from_z // 2) * 4 + lax.rem(x + event[1], 4)
-            for link, item in react(event):
-                dispatch(link, item, src, chip)
+                small.append(send(line, line, norm_sem.at[22 + k], norm_sem.at[9 + k], target["d"]))
         else:
             dz, dx = (1, event[1]) if kind == "z" else (event[1], event[2])
             chip = chip_at(dz, dx)
@@ -290,18 +270,19 @@
             for link, item in react(event):
                 dispatch(link, item, src, chip)
 
-    for dz in (0, 1):
-        for dx in range(4):
-            for chunk in range(N_CHUNKS):
-                arrived(place(chip_at(dz, dx), 1 - core, chunk), sib_sem.at[arrive_index(dz, dx, chunk)])
     for k in range(4):
         line = n_all.at[pl.ds((lax.rem(x + 4 - k, 4) * 2 + 1 - core) * 4, 4)]
         arrived(line, norm_sem.at[9 + k])
-    for copy in started:
+    for copy in small:
         copy.wait_send()
-
-
-def write_kernel(q_all, k_all, v_all, m_all, n_all, q_out, k_out, v_out, m_out, n_out, lines, sems):
+    for kind, per_piece in enumerate((4, 1, 1, 4)):
+        for side in (0, 1):
+            count = n_sent[kind][side]
+            waiting(many(kind, count), send_sem.at[kind * 2 + side], sib_sem.at[0]).wait_send()
+        arrived(many(kind, per_piece * 8), sib_sem.at[kind])
+
+
+def write_kernel(q_all, k_all, v_all, m_all, n_all, q_out, k_out, v_out, m_out, n_out, lines, rounded, sems):
     copies = []
     for k in range(8):
         copies.append((m_all.at[k], m_out.at[:, pl.ds(640 * k, 640)]))
@@ -323,7 +304,10 @@
             acc[q + 1] = jnp.where(lane < off + 40 - 128, turned, acc[q + 1])
     for q in range(5):
         lines[pl.ds(q, 8, stride=5), :] = acc[q]
-    n_out[...] = lines[...].astype(jnp.bfloat16)
+    rounded[...] = lines[...].astype(jnp.bfloat16)
+    last = pltpu.make_async_copy(rounded, n_out, sems.at[len(copies)])
+    last.start()
+    copies.append(last)
     for copy in copies:
         copy.wait()
 
@@ -349,10 +333,9 @@
         out_specs=[pl.BlockSpec(memory_space=vmem)] * 5,
         scratch_shapes=[pltpu.VMEM(a.shape, a.dtype) for a in args] + [
             pltpu.VMEM((320, 512), bf16), pltpu.VMEM((32, 320), bf16), pltpu.VMEM((4, 640, 128), f32),
-            pltpu.VMEM((2, 160, 1024), bf16), pltpu.VMEM((2, 320, 128), bf16), pltpu.VMEM((2, 4, 256, 640), bf16),
-            pltpu.SemaphoreType.DMA((N_LOADS,)), pltpu.SemaphoreType.DMA((N_SENDS,)),
-            pltpu.SemaphoreType.DMA((80,)), pltpu.SemaphoreType.DMA((22,)), pltpu.SemaphoreType.DMA((80,)),
-            pltpu.SemaphoreType.DMA((2,)), pltpu.SemaphoreType.DMA((13,)),
+            pltpu.SemaphoreType.DMA((N_LOADS,)), pltpu.SemaphoreType.DMA((8,)),
+            pltpu.SemaphoreType.DMA((80,)), pltpu.SemaphoreType.DMA((4,)),
+            pltpu.SemaphoreType.DMA((4,)), pltpu.SemaphoreType.DMA((26,)),
         ],
         compiler_params=pltpu.CompilerParams(
             collective_id=0, has_side_effects=True, vmem_limit_bytes=36 * 1024 * 1024
@@ -368,8 +351,8 @@
             jax.ShapeDtypeStruct((40, 128), bf16),
         ],
         in_specs=[pl.BlockSpec(memory_space=vmem)] * 5,
-        out_specs=[pl.BlockSpec(memory_space=hbm)] * 4 + [pl.BlockSpec(memory_space=vmem)],
-        scratch_shapes=[pltpu.VMEM((40, 128), f32), pltpu.SemaphoreType.DMA((18,))],
+        out_specs=[pl.BlockSpec(memory_space=hbm)] * 5,
+        scratch_shapes=[pltpu.VMEM((40, 128), f32), pltpu.VMEM((40, 128), bf16), pltpu.SemaphoreType.DMA((19,))],
         compiler_params=pltpu.CompilerParams(vmem_limit_bytes=2 * 1024 * 1024),
     )(q_all, k_all, v_all, m_all, n_all)
     return q, k, v, m, n.reshape(5120)

time: 99.6 us -> 96.8 us (0.972)
  Pallas kernels: 98.8 us -> 96 us
    pallas_call x1, Pallas kernels: 90.2 us -> 87.9 us  [body(): pl.pallas_call(gather_kernel, name='gather', out_shape=[vmem((5120, 1024)...]
where the time goes in v3:
time: 96.8 us; the launch traced here: 96.7 us
  Pallas kernels  96 us (99%)
    pallas_call x1, Pallas kernels, body(): pl.pallas_call(gather_kernel, name='gather', out_shape=[vmem((5120, 1024)...  87.9 us
    pallas_call x1, Pallas kernels, body(): pl.pallas_call(write_kernel, name='write', out_shape=[jax.ShapeDtypeStruc...  8.09 us

profile of v3, /device:TPU:1, one launch (start us, length us, event | category | flops | bytes accessed | tf_op | source)
XLA Modules:
  0.0 96.7 jit_solution(12692848042297879454)
XLA Ops:
  0.6 87.9 %gather.1 = (bf16[5120,1024]{1,0:T(8,128)(2,1)S(1)}, bf16[5120,128]{1,0:T(8,128)(2,1)S(1)}, bf16[5120,128]{1,0:T(8,128)(2,1)S(1)}, bf16[8,1024,640]{2,1,0:T(8,128)(2,1)S(1)}, f32[32,4,1,128]{3,2,1,0:T(1,128)S(1)}) custom-call(bf16[320,1024]{1,0:T(8,128)(2,1)} %tq.1, bf16[32,320]{1,0:T(8,128)(2,1)} %bitcast.10, bf16[32,1024]{1,0:T(8,128)(2,1)} %hq.1, ...), custom_call_target="tpu_custom_call" | custom-call | tf_op jit(solution)/shard_map/gather/pallas_call | solution.py:325
  88.6 8.1 %write.1 = (bf16[5120,1024]{1,0:T(8,128)(2,1)}, bf16[5120,128]{1,0:T(8,128)(2,1)}, bf16[5120,128]{1,0:T(8,128)(2,1)}, bf16[1024,5120]{1,0:T(8,128)(2,1)}, bf16[40,128]{1,0:T(8,128)(2,1)}) custom-call(bf16[5120,1024]{1,0:T(8,128)(2,1)S(1)} %get-tuple-element.15.q_all, bf16[5120,128]{1,0:T(8,128)(2,1)S(1)} %get-tuple-element.16.k_all, ...), custom_call_target="tpu_custom_call" | custom-call | tf_op jit(solution)/shard_map/write/pallas_call | solution.py:345

commit v4 on v3

--- a/solution.py
+++ b/solution.py
@@ -11,13 +11,13 @@
 MESH = pl.DeviceIdType.MESH
 mix_rate = 0.5
 
-Q_ROWS = 80
-M_ROWS = 128
-HALF = (0, 0, 0, 1, 1, 1, 0, 0, 1, 1)
-IS_B = (0,) * 6 + (1,) * 4
-SIZES = (163840, 163840, 81920, 163840, 163840, 81920) + (163840,) * 4
-N_CHUNKS = 10
-KIND = (0, 0, 1, 0, 0, 2, 3, 3, 3, 3)
+Q_ROWS = 160
+M_ROWS = 256
+HALF = (0, 0, 1, 1, 0, 1)
+IS_B = (0, 0, 0, 0, 1, 1)
+KIND = (0, 1, 0, 2, 3, 3)
+SIZES = (327680, 81920, 327680, 81920, 327680, 327680)
+N_CHUNKS = 6
 
 
 def own_sends(chunk, along_x, along_z):
@@ -53,17 +53,17 @@
 
 def plan():
     first = []
-    for chunk in (0, 3):
+    for chunk in (0,):
         first += own_sends(chunk, True, True)
     second = []
-    for chunk in (1, 4, 2, 5):
+    for chunk in (2, 1, 3):
         second += own_sends(chunk, False, True)
     third = []
-    for chunk in (6, 8, 7, 9):
+    for chunk in (4, 5):
         third += own_sends(chunk, True, True)
-    for chunk in (1, 4, 2, 5):
+    for chunk in (2, 1, 3):
         third += own_sends(chunk, True, False)
-    starts = [(2.0, first), (2.1, second), (6.0, third)]
+    starts = [(2.0, first), (2.2, second), (5.5, third)]
     heap, count, free, order = [], 0, {}, []
     for time, sends in starts:
         heapq.heappush(heap, (time, count, None, sends))
@@ -80,7 +80,7 @@
             free[link] = done
             heapq.heappush(heap, (done + 1.9, count, item, None))
             count += 1
-    order += [(9.0, ("ny",)), (32.0, ("nz",)), (56.0, ("nx",))]
+    order += [(t, (name,)) for t, name in ((9.0, "n0"), (38.0, "n1"), (64.0, "n2"), (67.5, "n3"), (71.0, "n4"), (74.0, "n5"))]
     order = [event for _, event in sorted(order, key=lambda pair: pair[0])]
     return first, second, third, order
 
@@ -114,8 +114,9 @@
         "x+": device(dx=1), "x-": device(dx=3), "z": device(dz=2), "d": device(other=True),
     }
 
-    partners = [device(dx=k) for k in (1, 2, 3)] + [device(dz=k) for k in (1, 2, 3)]
-    partners += [device(dy=k) for k in (1, 2, 3)] + [device(other=True)]
+    beside = device(dz=1 + 2 * lax.rem(z, 2))
+    partners = [device(dx=k) for k in (1, 2, 3)] + [beside, target["z"]]
+    partners += [device(dy=k) for k in (1, 3)] + [target["d"]]
     barrier = pltpu.get_barrier_semaphore()
     for partner in partners:
         pl.semaphore_signal(barrier, inc=1, device_id=partner, device_id_type=MESH)
@@ -151,18 +152,17 @@
             return q_all.at[pl.ds(0, Q_ROWS * count)]
         if kind < 3:
             return (k_all if kind == 1 else v_all).at[pl.ds(0, 320 * count)]
-        if count % 8 == 0:
-            return m_all.at[pl.ds(0, count // 8)]
-        return m_all.at[pl.ds(0, count // 4), pl.ds(0, 512)]
+        if count % 4 == 0:
+            return m_all.at[pl.ds(0, count // 4)]
+        return m_all.at[pl.ds(0, count // 2), pl.ds(0, 512)]
 
     def place(chip, cc, chunk):
         row = (chip * 2 + cc) * 320
-        if chunk in (2, 5):
-            return (k_all if chunk == 2 else v_all).at[pl.ds(pl.multiple_of(row, 64), 320)]
-        if chunk < 6:
-            part = chunk if chunk < 2 else chunk - 1
-            return q_all.at[pl.ds(pl.multiple_of(row + Q_ROWS * part, 16), Q_ROWS)]
-        return m_all.at[chip, pl.ds(pl.multiple_of(512 * cc + M_ROWS * (chunk - 6), M_ROWS), M_ROWS)]
+        if KIND[chunk] in (1, 2):
+            return (k_all if KIND[chunk] == 1 else v_all).at[pl.ds(pl.multiple_of(row, 64), 320)]
+        if KIND[chunk] == 0:
+            return q_all.at[pl.ds(pl.multiple_of(row + Q_ROWS * HALF[chunk], 32), Q_ROWS)]
+        return m_all.at[chip, pl.ds(pl.multiple_of(512 * cc + M_ROWS * HALF[chunk], M_ROWS), M_ROWS)]
 
     def chip_at(dz2, dx):
         return (lax.rem(sh // 8 + dz2, 2)) * 4 + lax.rem(x + dx, 4)
@@ -193,10 +193,28 @@
         )
 
     row = sh * 320
+    wait_loads(12, 13)
+    plane = core * 4 + y
+    n_all[plane, z, x] = jnp.zeros((1, 128), jnp.float32)
+    n_all[plane, z, x, :, 0:40] = n1_v[...] + n2_v[...]
     wait_loads(0, 1, 2)
     q_all[pl.ds(pl.multiple_of(row, 64), 320)] = (
         tq_v[...].astype(jnp.float32) + product(lq_v[...], hq_v[...])
     ).astype(jnp.bfloat16)
+    pl.semaphore_wait(barrier, len(partners))
+    line = n_all.at[plane, z, x]
+    small = [send(line, line, norm_sem.at[8 + k], norm_sem.at[k - 1], device(dx=k)) for k in (1, 2, 3)]
+    for link, item in first:
+        dispatch(link, item, place(own, core, item[-1]), own)
+
+    half = pl.ds(pl.multiple_of(512 * core, 512), 512)
+    other_half = pl.ds(pl.multiple_of(512 * (1 - core), 512), 512)
+    wait_loads(3, 4)
+    small += [
+        send(tm_v.at[:, other_half], tm_s, pair_sem.at[2], pair_sem.at[0], target["d"]),
+        send(hm_v, hm_s, pair_sem.at[3], pair_sem.at[1], target["d"]),
+    ]
+
     wait_loads(6, 7, 8, 9, 10, 11)
     k_all[pl.ds(pl.multiple_of(row, 64), 320)] = (
         tk_v[...].astype(jnp.float32) + product(lk_v[...], hk_v[...])
@@ -204,27 +222,10 @@
     v_all[pl.ds(pl.multiple_of(row, 64), 320)] = (
         tv_v[...].astype(jnp.float32) + product(lv_v[...], hv_v[...])
     ).astype(jnp.bfloat16)
-    wait_loads(12, 13)
-    n_at = (x * 2 + core) * 4 + z
-    n_all[n_at, y] = jnp.zeros((1, 128), jnp.float32)
-    n_all[n_at, y, :, 0:40] = n1_v[...] + n2_v[...]
-    wait_loads(3, 4, 5)
-    pl.semaphore_wait(barrier, len(partners))
-
-    half = pl.ds(pl.multiple_of(512 * core, 512), 512)
-    other_half = pl.ds(pl.multiple_of(512 * (1 - core), 512), 512)
-    small = [
-        send(tm_v.at[:, other_half], tm_s, pair_sem.at[2], pair_sem.at[0], target["d"]),
-        send(hm_v, hm_s, pair_sem.at[3], pair_sem.at[1], target["d"]),
-    ]
-    for link, item in first:
-        dispatch(link, item, place(own, core, item[-1]), own)
-    for k in (1, 2, 3):
-        line = n_all.at[n_at, y]
-        small.append(send(line, line, norm_sem.at[12 + k], norm_sem.at[k - 1], device(dy=k)))
     for link, item in second:
         dispatch(link, item, place(own, core, item[-1]), own)
 
+    wait_loads(5)
     arrived(tm_s, pair_sem.at[0])
     arrived(hm_s, pair_sem.at[1])
     mine = pl.ds(pl.multiple_of(320 * core, 64), 320)
@@ -232,36 +233,44 @@
     low_half = lm_v[:, half]
     own_half = tm_v[:, half]
     for b in range(4):
-        cols = slice(M_ROWS * b, M_ROWS * (b + 1))
+        cols = slice(128 * b, 128 * (b + 1))
         low = low_half[:, cols]
         turn[b, mine] = own_half[:, cols].astype(jnp.float32) + product(hm_v[...], low)
         turn[b, others] = tm_s[:, cols].astype(jnp.float32) + product(hm_s[...], low)
-        rows = pl.ds(pl.multiple_of(512 * core + M_ROWS * b, M_ROWS), M_ROWS)
+        rows = pl.ds(pl.multiple_of(512 * core + 128 * b, 128), 128)
         m_all[own, rows] = turn[b].T.astype(jnp.bfloat16)
     for link, item in third:
         dispatch(link, item, place(own, core, item[-1]), own)
 
     for event in order:
         kind, chunk = event[0], event[-1]
-        if kind == "ny":
+        if kind == "n0":
             for k in (1, 2, 3):
-                arrived(n_all.at[n_at, lax.rem(y + 4 - k, 4)], norm_sem.at[k - 1])
-            for k in (1, 2, 3):
-                line = n_all.at[n_at]
-                small.append(send(line, line, norm_sem.at[15 + k], norm_sem.at[3 + k - 1], device(dz=k)))
-        elif kind == "nz":
-            block = (x * 2 + core) * 4
-            for k in (1, 2, 3):
-                arrived(n_all.at[block + lax.rem(z + 4 - k, 4)], norm_sem.at[3 + k - 1])
-            line = n_all.at[pl.ds(block, 4)]
-            for k in (1, 2, 3):
-                small.append(send(line, line, norm_sem.at[18 + k], norm_sem.at[6 + k - 1], device(dx=k)))
-            small.append(send(line, line, norm_sem.at[22], norm_sem.at[9], target["d"]))
-        elif kind == "nx":
-            for k in (1, 2, 3):
-                line = n_all.at[pl.ds((lax.rem(x + 4 - k, 4) * 2 + core) * 4, 4)]
-                arrived(line, norm_sem.at[6 + k - 1])
-                small.append(send(line, line, norm_sem.at[22 + k], norm_sem.at[9 + k], target["d"]))
+                arrived(n_all.at[plane, z, lax.rem(x + 4 - k, 4)], norm_sem.at[k - 1])
+            line = n_all.at[plane, z]
+            small.append(send(line, line, norm_sem.at[12], norm_sem.at[3], beside))
+        elif kind == "n1":
+            arrived(n_all.at[plane, lax.rem(z + 1 + 2 * lax.rem(z, 2), 4)], norm_sem.at[3])
+            line = n_all.at[plane, pl.ds((z // 2) * 2, 2)]
+            small.append(send(line, line, norm_sem.at[13], norm_sem.at[4], target["z"]))
+        elif kind == "n2":
+            arrived(n_all.at[plane, pl.ds((1 - z // 2) * 2, 2)], norm_sem.at[4])
+            line = n_all.at[plane]
+            for k in (1, 3):
+                small.append(send(line, line, norm_sem.at[13 + k], norm_sem.at[4 + k], device(dy=k)))
+        elif kind == "n3":
+            for k in (1, 3):
+                arrived(n_all.at[core * 4 + lax.rem(y + 4 - k, 4)], norm_sem.at[4 + k])
+            line = n_all.at[core * 4 + lax.rem(y + 3, 4)]
+            small.append(send(line, line, norm_sem.at[15], norm_sem.at[6], device(dy=1)))
+        elif kind == "n4":
+            arrived(n_all.at[core * 4 + lax.rem(y + 2, 4)], norm_sem.at[6])
+            line = n_all.at[pl.ds(core * 4, 4)]
+            small.append(send(line, line, norm_sem.at[17], norm_sem.at[8], target["d"]))
+        elif kind == "n5":
+            arrived(n_all.at[pl.ds((1 - core) * 4, 4)], norm_sem.at[8])
+            for copy in small:
+                copy.wait_send()
         else:
             dz, dx = (1, event[1]) if kind == "z" else (event[1], event[2])
             chip = chip_at(dz, dx)
@@ -270,12 +279,7 @@
             for link, item in react(event):
                 dispatch(link, item, src, chip)
 
-    for k in range(4):
-        line = n_all.at[pl.ds((lax.rem(x + 4 - k, 4) * 2 + 1 - core) * 4, 4)]
-        arrived(line, norm_sem.at[9 + k])
-    for copy in small:
-        copy.wait_send()
-    for kind, per_piece in enumerate((4, 1, 1, 4)):
+    for kind, per_piece in enumerate((2, 1, 1, 2)):
         for side in (0, 1):
             count = n_sent[kind][side]
             waiting(many(kind, count), send_sem.at[kind * 2 + side], sib_sem.at[0]).wait_send()
@@ -295,7 +299,7 @@
     acc = [jnp.zeros((8, 128), jnp.float32) for _ in range(5)]
     for i in range(16):
         core, zl, y = i // 8, (i // 4) % 2, i % 4
-        rows = [n_all[(xx * 2 + core) * 4 + zh * 2 + zl, y] for zh in range(2) for xx in range(4)]
+        rows = [n_all[core * 4 + y, zh * 2 + zl, xx] for zh in range(2) for xx in range(4)]
         block = jnp.concatenate(rows, axis=0)
         q, off = (40 * i) // 128, (40 * i) % 128
         turned = pltpu.roll(block, off, 1) if off else block
@@ -327,15 +331,15 @@
         name="gather",
         out_shape=[
             vmem((5120, 1024), bf16), vmem((5120, 128), bf16), vmem((5120, 128), bf16),
-            vmem((8, 1024, 640), bf16), vmem((32, 4, 1, 128), f32),
+            vmem((8, 1024, 640), bf16), vmem((8, 4, 4, 1, 128), f32),
         ],
         in_specs=[pl.BlockSpec(memory_space=pltpu.MemorySpace.HBM)] * 14,
         out_specs=[pl.BlockSpec(memory_space=vmem)] * 5,
         scratch_shapes=[pltpu.VMEM(a.shape, a.dtype) for a in args] + [
             pltpu.VMEM((320, 512), bf16), pltpu.VMEM((32, 320), bf16), pltpu.VMEM((4, 640, 128), f32),
             pltpu.SemaphoreType.DMA((N_LOADS,)), pltpu.SemaphoreType.DMA((8,)),
-            pltpu.SemaphoreType.DMA((80,)), pltpu.SemaphoreType.DMA((4,)),
-            pltpu.SemaphoreType.DMA((4,)), pltpu.SemaphoreType.DMA((26,)),
+            pltpu.SemaphoreType.DMA((8 * N_CHUNKS,)), pltpu.SemaphoreType.DMA((4,)),
+            pltpu.SemaphoreType.DMA((4,)), pltpu.SemaphoreType.DMA((18,)),
         ],
         compiler_params=pltpu.CompilerParams(
             collective_id=0, has_side_effects=True, vmem_limit_bytes=36 * 1024 * 1024

time: 96.8 us -> 93.9 us (0.970)
  Pallas kernels: 96 us -> 93.2 us
    pallas_call x1, Pallas kernels: 87.9 us -> 85.1 us  [body(): pl.pallas_call(gather_kernel, name='gather', out_shape=[vmem((5120, 1024)...]
where the time goes in v4:
time: 93.9 us; the launch traced here: 93.8 us
  Pallas kernels  93.2 us (99%)
    pallas_call x1, Pallas kernels, body(): pl.pallas_call(gather_kernel, name='gather', out_shape=[vmem((5120, 1024)...  85.1 us
    pallas_call x1, Pallas kernels, body(): pl.pallas_call(write_kernel, name='write', out_shape=[jax.ShapeDtypeStruc...  8.1 us

profile of v4, /device:TPU:1, one launch (start us, length us, event | category | flops | bytes accessed | tf_op | source)
XLA Modules:
  0.0 93.8 jit_solution(12559582725213894683)
XLA Ops:
  0.6 85.1 %gather.1 = (bf16[5120,1024]{1,0:T(8,128)(2,1)S(1)}, bf16[5120,128]{1,0:T(8,128)(2,1)S(1)}, bf16[5120,128]{1,0:T(8,128)(2,1)S(1)}, bf16[8,1024,640]{2,1,0:T(8,128)(2,1)S(1)}, f32[8,4,4,1,128]{4,3,2,1,0:T(1,128)S(1)}) custom-call(bf16[320,1024]{1,0:T(8,128)(2,1)} %tq.1, bf16[32,320]{1,0:T(8,128)(2,1)} %bitcast.10, bf16[32,1024]{1,0:T(8,128)(2,1)} %hq.1, ...), custom_call_target="tpu_custom_call" | custom-call | tf_op jit(solution)/shard_map/gather/pallas_call | solution.py:329
  85.7 8.1 %write.1 = (bf16[5120,1024]{1,0:T(8,128)(2,1)}, bf16[5120,128]{1,0:T(8,128)(2,1)}, bf16[5120,128]{1,0:T(8,128)(2,1)}, bf16[1024,5120]{1,0:T(8,128)(2,1)}, bf16[40,128]{1,0:T(8,128)(2,1)}) custom-call(bf16[5120,1024]{1,0:T(8,128)(2,1)S(1)} %get-tuple-element.15.q_all, bf16[5120,128]{1,0:T(8,128)(2,1)S(1)} %get-tuple-element.16.k_all, ...), custom_call_target="tpu_custom_call" | custom-call | tf_op jit(solution)/shard_map/write/pallas_call | solution.py:349

commit v5 on v4

--- a/solution.py
+++ b/solution.py
@@ -13,11 +13,12 @@
 
 Q_ROWS = 160
 M_ROWS = 256
-HALF = (0, 0, 1, 1, 0, 1)
-IS_B = (0, 0, 0, 0, 1, 1)
-KIND = (0, 1, 0, 2, 3, 3)
-SIZES = (327680, 81920, 327680, 81920, 327680, 327680)
-N_CHUNKS = 6
+KIND = (0, 1, 0, 2, 3, 3, 0, 3, 3, 3)
+FROM = (0, 0, 1, 0, 0, 1, 0, 0, 1, 1.75)
+WEIGHT = (1, 1, 1, 1, 1, 1, 2, 2, 0.75, 0.25)
+SIZES = (327680, 81920, 327680, 81920, 327680, 327680, 655360, 655360, 245760, 81920)
+ONWARD = {"x+": {6: 0, 0: 0, 1: 1, 7: 4}, "x-": {6: 2, 2: 2, 3: 3, 7: 5}}
+PARTNERS = {"x+": (0, 1, 2, 3), "x-": (2, 3, 0, 1)}
 
 
 def own_sends(chunk, along_x, along_z):
@@ -35,33 +36,30 @@
     kind = event[0]
     if kind == "z":
         _, dx, chunk = event
-        sends = [("d", ("d", 1, dx, chunk))]
-        if not IS_B[chunk]:
-            sends += [("x+", ("x+", 1, 3, chunk)), ("x-", ("x-", 1, 1, chunk))]
-        return sends
+        return [("d", ("d", 1, dx, chunk))]
     _, dz, dx, chunk = event
     sends = []
-    if kind == "x+" and dx == 3 and HALF[chunk] == 0:
-        sends.append(("x+", ("x+", dz, 2, chunk)))
-    if kind == "x-" and dx == 1 and HALF[chunk] == 1:
-        sends.append(("x-", ("x-", dz, 2, chunk)))
-    if IS_B[chunk] and dz == 0:
-        sends.append(("z", ("z", dx, chunk)))
+    if dx != 2 and chunk in ONWARD[kind]:
+        sends.append((kind, (kind, dz, 2, ONWARD[kind][chunk])))
+        if (dz, chunk) == (0, 7):
+            sends += [(kind, (kind, 1, dx, other)) for other in PARTNERS[kind]]
+    if KIND[chunk] == 3 and dz == 0:
+        sends += [("z", ("z", dx, part)) for part in ((8, 9) if chunk == 5 else (chunk,))]
     sends.append(("d", ("d", dz, dx, chunk)))
     return sends
 
 
 def plan():
     first = []
-    for chunk in (0,):
+    for chunk in (6,):
         first += own_sends(chunk, True, True)
     second = []
-    for chunk in (2, 1, 3):
+    for chunk in (1, 3):
         second += own_sends(chunk, False, True)
     third = []
-    for chunk in (4, 5):
+    for chunk in (7,):
         third += own_sends(chunk, True, True)
-    for chunk in (2, 1, 3):
+    for chunk in (1, 3):
         third += own_sends(chunk, True, False)
     starts = [(2.0, first), (2.2, second), (5.5, third)]
     heap, count, free, order = [], 0, {}, []
@@ -82,9 +80,21 @@
             count += 1
     order += [(t, (name,)) for t, name in ((9.0, "n0"), (38.0, "n1"), (64.0, "n2"), (67.5, "n3"), (71.0, "n4"), (74.0, "n5"))]
     order = [event for _, event in sorted(order, key=lambda pair: pair[0])]
+    held = [order.index(("x+", 0, 3, 7)), order.index(("x-", 0, 1, 7))]
+    assert min(held) > max(order.index(("z", 0, chunk)) for chunk in (6, 1, 3))
     return first, second, third, order
 
 
+def slots():
+    found = {}
+    for event in plan()[3]:
+        if event[0][0] != "n":
+            dz, dx = (1, event[1]) if event[0] == "z" else (event[1], event[2])
+            found[(dz, dx, event[-1])] = len(found)
+    return found
+
+
+SLOTS = slots()
 N_LOADS = 14
 
 
@@ -161,14 +171,16 @@
         if KIND[chunk] in (1, 2):
             return (k_all if KIND[chunk] == 1 else v_all).at[pl.ds(pl.multiple_of(row, 64), 320)]
         if KIND[chunk] == 0:
-            return q_all.at[pl.ds(pl.multiple_of(row + Q_ROWS * HALF[chunk], 32), Q_ROWS)]
-        return m_all.at[chip, pl.ds(pl.multiple_of(512 * cc + M_ROWS * HALF[chunk], M_ROWS), M_ROWS)]
+            return q_all.at[pl.ds(pl.multiple_of(row + Q_ROWS * FROM[chunk], 32), Q_ROWS * WEIGHT[chunk])]
+        return m_all.at[
+            chip, pl.ds(pl.multiple_of(512 * cc + int(M_ROWS * FROM[chunk]), 64), int(M_ROWS * WEIGHT[chunk]))
+        ]
 
     def chip_at(dz2, dx):
         return (lax.rem(sh // 8 + dz2, 2)) * 4 + lax.rem(x + dx, 4)
 
     def arrive_index(dz, dx, chunk):
-        return (dz * 4 + dx) * N_CHUNKS + chunk
+        return SLOTS[(dz, dx, chunk)]
 
     def dispatch(link, item, src, chip):
         kind, chunk = KIND[item[-1]], item[-1]
@@ -177,7 +189,7 @@
         else:
             dz, dx = (1, item[1]) if link == "z" else (item[1], item[2])
             sem, side = arrive_sem.at[arrive_index(dz, dx, chunk)], 0
-        n_sent[kind][side] += 1
+        n_sent[kind][side] += WEIGHT[chunk]
         send(src, src, send_sem.at[kind * 2 + side], sem, target[link])
 
     first, second, third, order = plan()
@@ -277,11 +289,12 @@
             src = place(chip, core, chunk)
             arrived(src, arrive_sem.at[arrive_index(dz, dx, chunk)])
             for link, item in react(event):
-                dispatch(link, item, src, chip)
+                at = chip_at(1, 0) if dz == 0 and item[0] == kind and item[1] == 1 else chip
+                dispatch(link, item, place(at, core, item[-1]), at)
 
     for kind, per_piece in enumerate((2, 1, 1, 2)):
         for side in (0, 1):
-            count = n_sent[kind][side]
+            count = int(n_sent[kind][side])
             waiting(many(kind, count), send_sem.at[kind * 2 + side], sib_sem.at[0]).wait_send()
         arrived(many(kind, per_piece * 8), sib_sem.at[kind])
 
@@ -338,7 +351,7 @@
         scratch_shapes=[pltpu.VMEM(a.shape, a.dtype) for a in args] + [
             pltpu.VMEM((320, 512), bf16), pltpu.VMEM((32, 320), bf16), pltpu.VMEM((4, 640, 128), f32),
             pltpu.SemaphoreType.DMA((N_LOADS,)), pltpu.SemaphoreType.DMA((8,)),
-            pltpu.SemaphoreType.DMA((8 * N_CHUNKS,)), pltpu.SemaphoreType.DMA((4,)),
+            pltpu.SemaphoreType.DMA((len(SLOTS),)), pltpu.SemaphoreType.DMA((4,)),
             pltpu.SemaphoreType.DMA((4,)), pltpu.SemaphoreType.DMA((18,)),
         ],
         compiler_params=pltpu.CompilerParams(

time: 93.9 us -> 93.9 us (level)
  no operation moved by 1% of the time
where the time goes in v5:
time: 93.9 us; the launch traced here: 93.7 us
  Pallas kernels  93.1 us (99%)
    pallas_call x1, Pallas kernels, body(): pl.pallas_call(gather_kernel, name='gather', out_shape=[vmem((5120, 1024)...  85 us
    pallas_call x1, Pallas kernels, body(): pl.pallas_call(write_kernel, name='write', out_shape=[jax.ShapeDtypeStruc...  8.1 us

profile of v5, /device:TPU:1, one launch (start us, length us, event | category | flops | bytes accessed | tf_op | source)
XLA Modules:
  0.0 93.7 jit_solution(5968506873660264992)
XLA Ops:
  0.6 85.0 %gather.1 = (bf16[5120,1024]{1,0:T(8,128)(2,1)S(1)}, bf16[5120,128]{1,0:T(8,128)(2,1)S(1)}, bf16[5120,128]{1,0:T(8,128)(2,1)S(1)}, bf16[8,1024,640]{2,1,0:T(8,128)(2,1)S(1)}, f32[8,4,4,1,128]{4,3,2,1,0:T(1,128)S(1)}) custom-call(bf16[320,1024]{1,0:T(8,128)(2,1)} %tq.1, bf16[32,320]{1,0:T(8,128)(2,1)} %bitcast.10, bf16[32,1024]{1,0:T(8,128)(2,1)} %hq.1, ...), custom_call_target="tpu_custom_call" | custom-call | tf_op jit(solution)/shard_map/gather/pallas_call | solution.py:342
  85.6 8.1 %write.1 = (bf16[5120,1024]{1,0:T(8,128)(2,1)}, bf16[5120,128]{1,0:T(8,128)(2,1)}, bf16[5120,128]{1,0:T(8,128)(2,1)}, bf16[1024,5120]{1,0:T(8,128)(2,1)}, bf16[40,128]{1,0:T(8,128)(2,1)}) custom-call(bf16[5120,1024]{1,0:T(8,128)(2,1)S(1)} %get-tuple-element.15.q_all, bf16[5120,128]{1,0:T(8,128)(2,1)S(1)} %get-tuple-element.16.k_all, ...), custom_call_target="tpu_custom_call" | custom-call | tf_op jit(solution)/shard_map/write/pallas_call | solution.py:362

commit v6 on v5

--- a/solution.py
+++ b/solution.py
@@ -78,7 +78,7 @@
             free[link] = done
             heapq.heappush(heap, (done + 1.9, count, item, None))
             count += 1
-    order += [(t, (name,)) for t, name in ((9.0, "n0"), (38.0, "n1"), (64.0, "n2"), (67.5, "n3"), (71.0, "n4"), (74.0, "n5"))]
+    order += [(t, (name,)) for t, name in ((30.0, "n1"), (42.0, "n2"), (45.0, "n3"), (48.0, "n4"), (51.0, "n5"), (60.0, "n6"))]
     order = [event for _, event in sorted(order, key=lambda pair: pair[0])]
     held = [order.index(("x+", 0, 3, 7)), order.index(("x-", 0, 1, 7))]
     assert min(held) > max(order.index(("z", 0, chunk)) for chunk in (6, 1, 3))
@@ -125,11 +125,18 @@
     }
 
     beside = device(dz=1 + 2 * lax.rem(z, 2))
-    partners = [device(dx=k) for k in (1, 2, 3)] + [beside, target["z"]]
-    partners += [device(dy=k) for k in (1, 3)] + [target["d"]]
+    pair = device(dy=1 + 2 * lax.rem(y, 2))
+    inner = lax.rem((y + 1) // 2, 2)
+    across = device(dy=7 - 2 * y)
+    partners = [device(dx=k) for k in (1, 2, 3)] + [beside, target["z"], pair, target["d"]]
     barrier = pltpu.get_barrier_semaphore()
     for partner in partners:
         pl.semaphore_signal(barrier, inc=1, device_id=partner, device_id_type=MESH)
+
+    @pl.when(inner == 1)
+    def _():
+        pl.semaphore_signal(barrier, inc=1, device_id=across, device_id_type=MESH)
+
 
     loads = []
     for k, (src, dst) in enumerate((
@@ -213,7 +220,7 @@
     q_all[pl.ds(pl.multiple_of(row, 64), 320)] = (
         tq_v[...].astype(jnp.float32) + product(lq_v[...], hq_v[...])
     ).astype(jnp.bfloat16)
-    pl.semaphore_wait(barrier, len(partners))
+    pl.semaphore_wait(barrier, len(partners) + inner)
     line = n_all.at[plane, z, x]
     small = [send(line, line, norm_sem.at[8 + k], norm_sem.at[k - 1], device(dx=k)) for k in (1, 2, 3)]
     for link, item in first:
@@ -251,36 +258,53 @@
         turn[b, others] = tm_s[:, cols].astype(jnp.float32) + product(hm_s[...], low)
         rows = pl.ds(pl.multiple_of(512 * core + 128 * b, 128), 128)
         m_all[own, rows] = turn[b].T.astype(jnp.bfloat16)
+    for k in (1, 2, 3):
+        arrived(n_all.at[plane, z, lax.rem(x + 4 - k, 4)], norm_sem.at[k - 1])
+    line = n_all.at[plane, z]
+    small.append(send(line, line, norm_sem.at[12], norm_sem.at[3], beside))
     for link, item in third:
         dispatch(link, item, place(own, core, item[-1]), own)
 
     for event in order:
         kind, chunk = event[0], event[-1]
-        if kind == "n0":
-            for k in (1, 2, 3):
-                arrived(n_all.at[plane, z, lax.rem(x + 4 - k, 4)], norm_sem.at[k - 1])
-            line = n_all.at[plane, z]
-            small.append(send(line, line, norm_sem.at[12], norm_sem.at[3], beside))
-        elif kind == "n1":
+        if kind == "n1":
             arrived(n_all.at[plane, lax.rem(z + 1 + 2 * lax.rem(z, 2), 4)], norm_sem.at[3])
             line = n_all.at[plane, pl.ds((z // 2) * 2, 2)]
             small.append(send(line, line, norm_sem.at[13], norm_sem.at[4], target["z"]))
         elif kind == "n2":
             arrived(n_all.at[plane, pl.ds((1 - z // 2) * 2, 2)], norm_sem.at[4])
             line = n_all.at[plane]
-            for k in (1, 3):
-                small.append(send(line, line, norm_sem.at[13 + k], norm_sem.at[4 + k], device(dy=k)))
+            small.append(send(line, line, norm_sem.at[14], norm_sem.at[5], pair))
         elif kind == "n3":
-            for k in (1, 3):
-                arrived(n_all.at[core * 4 + lax.rem(y + 4 - k, 4)], norm_sem.at[4 + k])
-            line = n_all.at[core * 4 + lax.rem(y + 3, 4)]
-            small.append(send(line, line, norm_sem.at[15], norm_sem.at[6], device(dy=1)))
+            arrived(n_all.at[core * 4 + y + 1 - 2 * lax.rem(y, 2)], norm_sem.at[5])
+            near = n_all.at[pl.ds(core * 4 + (y // 2) * 2, 2)]
+            far = n_all.at[pl.ds(core * 4 + (1 - y // 2) * 2, 2)]
+
+            @pl.when(inner == 1)
+            def _():
+                send(near, near, norm_sem.at[15], norm_sem.at[6], across)
         elif kind == "n4":
-            arrived(n_all.at[core * 4 + lax.rem(y + 2, 4)], norm_sem.at[6])
+
+            @pl.when(inner == 1)
+            def _():
+                arrived(far, norm_sem.at[6])
+                send(far, far, norm_sem.at[16], norm_sem.at[7], pair)
+        elif kind == "n5":
+
+            @pl.when(inner == 0)
+            def _():
+                arrived(far, norm_sem.at[7])
+
             line = n_all.at[pl.ds(core * 4, 4)]
             small.append(send(line, line, norm_sem.at[17], norm_sem.at[8], target["d"]))
-        elif kind == "n5":
+        elif kind == "n6":
             arrived(n_all.at[pl.ds((1 - core) * 4, 4)], norm_sem.at[8])
+
+            @pl.when(inner == 1)
+            def _():
+                waiting(near, norm_sem.at[15], norm_sem.at[6]).wait_send()
+                waiting(far, norm_sem.at[16], norm_sem.at[7]).wait_send()
+
             for copy in small:
                 copy.wait_send()
         else:

time: 93.9 us -> 93.9 us (level)
  no operation moved by 1% of the time
where the time goes in v6:
time: 93.9 us; the launch traced here: 93.7 us
  Pallas kernels  93.1 us (99%)
    pallas_call x1, Pallas kernels, body(): pl.pallas_call(gather_kernel, name='gather', out_shape=[vmem((5120, 1024)...  85 us
    pallas_call x1, Pallas kernels, body(): pl.pallas_call(write_kernel, name='write', out_shape=[jax.ShapeDtypeStruc...  8.1 us

profile of v6, /device:TPU:1, one launch (start us, length us, event | category | flops | bytes accessed | tf_op | source)
XLA Modules:
  0.0 93.7 jit_solution(13512731607373242127)
XLA Ops:
  0.6 85.0 %gather.1 = (bf16[5120,1024]{1,0:T(8,128)(2,1)S(1)}, bf16[5120,128]{1,0:T(8,128)(2,1)S(1)}, bf16[5120,128]{1,0:T(8,128)(2,1)S(1)}, bf16[8,1024,640]{2,1,0:T(8,128)(2,1)S(1)}, f32[8,4,4,1,128]{4,3,2,1,0:T(1,128)S(1)}) custom-call(bf16[320,1024]{1,0:T(8,128)(2,1)} %tq.1, bf16[32,320]{1,0:T(8,128)(2,1)} %bitcast.10, bf16[32,1024]{1,0:T(8,128)(2,1)} %hq.1, ...), custom_call_target="tpu_custom_call" | custom-call | tf_op jit(solution)/shard_map/gather/pallas_call | solution.py:366
  85.6 8.1 %write.1 = (bf16[5120,1024]{1,0:T(8,128)(2,1)}, bf16[5120,128]{1,0:T(8,128)(2,1)}, bf16[5120,128]{1,0:T(8,128)(2,1)}, bf16[1024,5120]{1,0:T(8,128)(2,1)}, bf16[40,128]{1,0:T(8,128)(2,1)}) custom-call(bf16[5120,1024]{1,0:T(8,128)(2,1)S(1)} %get-tuple-element.15.q_all, bf16[5120,128]{1,0:T(8,128)(2,1)S(1)} %get-tuple-element.16.k_all, ...), custom_call_target="tpu_custom_call" | custom-call | tf_op jit(solution)/shard_map/write/pallas_call | solution.py:386

commit v7 on v6

--- a/solution.py
+++ b/solution.py
@@ -124,6 +124,16 @@
         "x+": device(dx=1), "x-": device(dx=3), "z": device(dz=2), "d": device(other=True),
     }
 
+    loads = [
+        pltpu.make_async_copy(src, dst, load_sem.at[k])
+        for k, (src, dst) in enumerate((
+            (lq, lq_v), (hq, hq_v), (tq, tq_v), (n1, n1_v), (n2, n2_v), (tm, tm_v), (hm, hm_v), (lm, lm_v),
+            (tk, tk_v), (lk, lk_v), (hk, hk_v), (tv, tv_v), (lv, lv_v), (hv, hv_v),
+        ))
+    ]
+    for copy in loads[:5]:
+        copy.start()
+
     beside = device(dz=1 + 2 * lax.rem(z, 2))
     pair = device(dy=1 + 2 * lax.rem(y, 2))
     inner = lax.rem((y + 1) // 2, 2)
@@ -138,14 +148,8 @@
         pl.semaphore_signal(barrier, inc=1, device_id=across, device_id_type=MESH)
 
 
-    loads = []
-    for k, (src, dst) in enumerate((
-        (tq, tq_v), (lq, lq_v), (hq, hq_v), (tm, tm_v), (hm, hm_v), (lm, lm_v), (tk, tk_v), (lk, lk_v), (hk, hk_v),
-        (tv, tv_v), (lv, lv_v), (hv, hv_v), (n1, n1_v), (n2, n2_v),
-    )):
-        copy = pltpu.make_async_copy(src, dst, load_sem.at[k])
+    for copy in loads[5:]:
         copy.start()
-        loads.append(copy)
 
     def send(src, dst, sent, sem, to):
         copy = pltpu.make_async_remote_copy(
@@ -212,7 +216,7 @@
         )
 
     row = sh * 320
-    wait_loads(12, 13)
+    wait_loads(3, 4)
     plane = core * 4 + y
     n_all[plane, z, x] = jnp.zeros((1, 128), jnp.float32)
     n_all[plane, z, x, :, 0:40] = n1_v[...] + n2_v[...]
@@ -228,13 +232,13 @@
 
     half = pl.ds(pl.multiple_of(512 * core, 512), 512)
     other_half = pl.ds(pl.multiple_of(512 * (1 - core), 512), 512)
-    wait_loads(3, 4)
+    wait_loads(5, 6)
     small += [
         send(tm_v.at[:, other_half], tm_s, pair_sem.at[2], pair_sem.at[0], target["d"]),
         send(hm_v, hm_s, pair_sem.at[3], pair_sem.at[1], target["d"]),
     ]
 
-    wait_loads(6, 7, 8, 9, 10, 11)
+    wait_loads(8, 9, 10, 11, 12, 13)
     k_all[pl.ds(pl.multiple_of(row, 64), 320)] = (
         tk_v[...].astype(jnp.float32) + product(lk_v[...], hk_v[...])
     ).astype(jnp.bfloat16)
@@ -244,7 +248,7 @@
     for link, item in second:
         dispatch(link, item, place(own, core, item[-1]), own)
 
-    wait_loads(5)
+    wait_loads(7)
     arrived(tm_s, pair_sem.at[0])
     arrived(hm_s, pair_sem.at[1])
     mine = pl.ds(pl.multiple_of(320 * core, 64), 320)
@@ -327,7 +331,8 @@
     copies = []
     for k in range(8):
         copies.append((m_all.at[k], m_out.at[:, pl.ds(640 * k, 640)]))
-        copies.append((q_all.at[pl.ds(640 * k, 640)], q_out.at[pl.ds(640 * k, 640)]))
+        if k % 4 == 0:
+            copies.append((q_all.at[pl.ds(640 * k, 2560)], q_out.at[pl.ds(640 * k, 2560)]))
     copies += [(k_all, k_out), (v_all, v_out)]
     copies = [pltpu.make_async_copy(src, dst, sems.at[k]) for k, (src, dst) in enumerate(copies)]
     for copy in copies:
@@ -393,7 +398,7 @@
         ],
         in_specs=[pl.BlockSpec(memory_space=vmem)] * 5,
         out_specs=[pl.BlockSpec(memory_space=hbm)] * 5,
-        scratch_shapes=[pltpu.VMEM((40, 128), f32), pltpu.VMEM((40, 128), bf16), pltpu.SemaphoreType.DMA((19,))],
+        scratch_shapes=[pltpu.VMEM((40, 128), f32), pltpu.VMEM((40, 128), bf16), pltpu.SemaphoreType.DMA((13,))],
         compiler_params=pltpu.CompilerParams(vmem_limit_bytes=2 * 1024 * 1024),
     )(q_all, k_all, v_all, m_all, n_all)
     return q, k, v, m, n.reshape(5120)

time: 93.9 us -> 93.8 us (level)
  no operation moved by 1% of the time
where the time goes in v7:
time: 93.8 us; the launch traced here: 93.7 us
  Pallas kernels  93.1 us (99%)
    pallas_call x1, Pallas kernels, body(): pl.pallas_call(gather_kernel, name='gather', out_shape=[vmem((5120, 1024)...  85 us
    pallas_call x1, Pallas kernels, body(): pl.pallas_call(write_kernel, name='write', out_shape=[jax.ShapeDtypeStruc...  8.08 us

profile of v7, /device:TPU:1, one launch (start us, length us, event | category | flops | bytes accessed | tf_op | source)
XLA Modules:
  0.0 93.7 jit_solution(13778322680011825412)
XLA Ops:
  0.6 85.0 %gather.1 = (bf16[5120,1024]{1,0:T(8,128)(2,1)S(1)}, bf16[5120,128]{1,0:T(8,128)(2,1)S(1)}, bf16[5120,128]{1,0:T(8,128)(2,1)S(1)}, bf16[8,1024,640]{2,1,0:T(8,128)(2,1)S(1)}, f32[8,4,4,1,128]{4,3,2,1,0:T(1,128)S(1)}) custom-call(bf16[320,1024]{1,0:T(8,128)(2,1)} %tq.1, bf16[32,320]{1,0:T(8,128)(2,1)} %bitcast.10, bf16[32,1024]{1,0:T(8,128)(2,1)} %hq.1, ...), custom_call_target="tpu_custom_call" | custom-call | tf_op jit(solution)/shard_map/gather/pallas_call | solution.py:371
  85.6 8.1 %write.1 = (bf16[5120,1024]{1,0:T(8,128)(2,1)}, bf16[5120,128]{1,0:T(8,128)(2,1)}, bf16[5120,128]{1,0:T(8,128)(2,1)}, bf16[1024,5120]{1,0:T(8,128)(2,1)}, bf16[40,128]{1,0:T(8,128)(2,1)}) custom-call(bf16[5120,1024]{1,0:T(8,128)(2,1)S(1)} %get-tuple-element.15.q_all, bf16[5120,128]{1,0:T(8,128)(2,1)S(1)} %get-tuple-element.16.k_all, ...), custom_call_target="tpu_custom_call" | custom-call | tf_op jit(solution)/shard_map/write/pallas_call | solution.py:391

commit v8 on v7

--- a/solution.py
+++ b/solution.py
@@ -138,7 +138,7 @@
     pair = device(dy=1 + 2 * lax.rem(y, 2))
     inner = lax.rem((y + 1) // 2, 2)
     across = device(dy=7 - 2 * y)
-    partners = [device(dx=k) for k in (1, 2, 3)] + [beside, target["z"], pair, target["d"]]
+    partners = [target["z"]] + [device(dx=k) for k in (3, 1, 2)] + [beside, pair, target["d"]]
     barrier = pltpu.get_barrier_semaphore()
     for partner in partners:
         pl.semaphore_signal(barrier, inc=1, device_id=partner, device_id_type=MESH)
@@ -226,7 +226,10 @@
     ).astype(jnp.bfloat16)
     pl.semaphore_wait(barrier, len(partners) + inner)
     line = n_all.at[plane, z, x]
-    small = [send(line, line, norm_sem.at[8 + k], norm_sem.at[k - 1], device(dx=k)) for k in (1, 2, 3)]
+    for k in (1, 2, 3):
+        send(line, line, norm_sem.at[1], norm_sem.at[0], device(dx=k))
+    three = n_all.at[plane, z, pl.ds(0, 3)]
+    small = [waiting(three, norm_sem.at[1], norm_sem.at[0])]
     for link, item in first:
         dispatch(link, item, place(own, core, item[-1]), own)
 
@@ -262,52 +265,51 @@
         turn[b, others] = tm_s[:, cols].astype(jnp.float32) + product(hm_s[...], low)
         rows = pl.ds(pl.multiple_of(512 * core + 128 * b, 128), 128)
         m_all[own, rows] = turn[b].T.astype(jnp.bfloat16)
-    for k in (1, 2, 3):
-        arrived(n_all.at[plane, z, lax.rem(x + 4 - k, 4)], norm_sem.at[k - 1])
+    arrived(three, norm_sem.at[0])
     line = n_all.at[plane, z]
-    small.append(send(line, line, norm_sem.at[12], norm_sem.at[3], beside))
+    small.append(send(line, line, norm_sem.at[8], norm_sem.at[2], beside))
     for link, item in third:
         dispatch(link, item, place(own, core, item[-1]), own)
 
     for event in order:
         kind, chunk = event[0], event[-1]
         if kind == "n1":
-            arrived(n_all.at[plane, lax.rem(z + 1 + 2 * lax.rem(z, 2), 4)], norm_sem.at[3])
+            arrived(n_all.at[plane, lax.rem(z + 1 + 2 * lax.rem(z, 2), 4)], norm_sem.at[2])
             line = n_all.at[plane, pl.ds((z // 2) * 2, 2)]
-            small.append(send(line, line, norm_sem.at[13], norm_sem.at[4], target["z"]))
+            small.append(send(line, line, norm_sem.at[9], norm_sem.at[3], target["z"]))
         elif kind == "n2":
-            arrived(n_all.at[plane, pl.ds((1 - z // 2) * 2, 2)], norm_sem.at[4])
+            arrived(n_all.at[plane, pl.ds((1 - z // 2) * 2, 2)], norm_sem.at[3])
             line = n_all.at[plane]
-            small.append(send(line, line, norm_sem.at[14], norm_sem.at[5], pair))
+            small.append(send(line, line, norm_sem.at[10], norm_sem.at[4], pair))
         elif kind == "n3":
-            arrived(n_all.at[core * 4 + y + 1 - 2 * lax.rem(y, 2)], norm_sem.at[5])
+            arrived(n_all.at[core * 4 + y + 1 - 2 * lax.rem(y, 2)], norm_sem.at[4])
             near = n_all.at[pl.ds(core * 4 + (y // 2) * 2, 2)]
             far = n_all.at[pl.ds(core * 4 + (1 - y // 2) * 2, 2)]
 
             @pl.when(inner == 1)
             def _():
-                send(near, near, norm_sem.at[15], norm_sem.at[6], across)
+                send(near, near, norm_sem.at[11], norm_sem.at[5], across)
         elif kind == "n4":
 
             @pl.when(inner == 1)
             def _():
-                arrived(far, norm_sem.at[6])
-                send(far, far, norm_sem.at[16], norm_sem.at[7], pair)
+                arrived(far, norm_sem.at[5])
+                send(far, far, norm_sem.at[12], norm_sem.at[6], pair)
         elif kind == "n5":
 
             @pl.when(inner == 0)
             def _():
-                arrived(far, norm_sem.at[7])
+                arrived(far, norm_sem.at[6])
 
             line = n_all.at[pl.ds(core * 4, 4)]
-            small.append(send(line, line, norm_sem.at[17], norm_sem.at[8], target["d"]))
+            small.append(send(line, line, norm_sem.at[13], norm_sem.at[7], target["d"]))
         elif kind == "n6":
-            arrived(n_all.at[pl.ds((1 - core) * 4, 4)], norm_sem.at[8])
+            arrived(n_all.at[pl.ds((1 - core) * 4, 4)], norm_sem.at[7])
 
             @pl.when(inner == 1)
             def _():
-                waiting(near, norm_sem.at[15], norm_sem.at[6]).wait_send()
-                waiting(far, norm_sem.at[16], norm_sem.at[7]).wait_send()
+                waiting(near, norm_sem.at[11], norm_sem.at[5]).wait_send()
+                waiting(far, norm_sem.at[12], norm_sem.at[6]).wait_send()
 
             for copy in small:
                 copy.wait_send()
@@ -381,7 +383,7 @@
             pltpu.VMEM((320, 512), bf16), pltpu.VMEM((32, 320), bf16), pltpu.VMEM((4, 640, 128), f32),
             pltpu.SemaphoreType.DMA((N_LOADS,)), pltpu.SemaphoreType.DMA((8,)),
             pltpu.SemaphoreType.DMA((len(SLOTS),)), pltpu.SemaphoreType.DMA((4,)),
-            pltpu.SemaphoreType.DMA((4,)), pltpu.SemaphoreType.DMA((18,)),
+            pltpu.SemaphoreType.DMA((4,)), pltpu.SemaphoreType.DMA((14,)),
         ],
         compiler_params=pltpu.CompilerParams(
             collective_id=0, has_side_effects=True, vmem_limit_bytes=36 * 1024 * 1024

time: 93.8 us -> 93.8 us (level)
  no operation moved by 1% of the time
where the time goes in v8:
time: 93.8 us; the launch traced here: 93.7 us
  Pallas kernels  93.1 us (99%)
    pallas_call x1, Pallas kernels, body(): pl.pallas_call(gather_kernel, name='gather', out_shape=[vmem((5120, 1024)...  85 us
    pallas_call x1, Pallas kernels, body(): pl.pallas_call(write_kernel, name='write', out_shape=[jax.ShapeDtypeStruc...  8.08 us

profile of v8, /device:TPU:1, one launch (start us, length us, event | category | flops | bytes accessed | tf_op | source)
XLA Modules:
  0.0 93.7 jit_solution(14540768068718280133)
XLA Ops:
  0.6 85.0 %gather.1 = (bf16[5120,1024]{1,0:T(8,128)(2,1)S(1)}, bf16[5120,128]{1,0:T(8,128)(2,1)S(1)}, bf16[5120,128]{1,0:T(8,128)(2,1)S(1)}, bf16[8,1024,640]{2,1,0:T(8,128)(2,1)S(1)}, f32[8,4,4,1,128]{4,3,2,1,0:T(1,128)S(1)}) custom-call(bf16[320,1024]{1,0:T(8,128)(2,1)} %tq.1, bf16[32,320]{1,0:T(8,128)(2,1)} %bitcast.10, bf16[32,1024]{1,0:T(8,128)(2,1)} %hq.1, ...), custom_call_target="tpu_custom_call" | custom-call | tf_op jit(solution)/shard_map/gather/pallas_call | solution.py:373
  85.6 8.1 %write.1 = (bf16[5120,1024]{1,0:T(8,128)(2,1)}, bf16[5120,128]{1,0:T(8,128)(2,1)}, bf16[5120,128]{1,0:T(8,128)(2,1)}, bf16[1024,5120]{1,0:T(8,128)(2,1)}, bf16[40,128]{1,0:T(8,128)(2,1)}) custom-call(bf16[5120,1024]{1,0:T(8,128)(2,1)S(1)} %get-tuple-element.15.q_all, bf16[5120,128]{1,0:T(8,128)(2,1)S(1)} %get-tuple-element.16.k_all, ...), custom_call_target="tpu_custom_call" | custom-call | tf_op jit(solution)/shard_map/write/pallas_call | solution.py:393
